TPU v7x, 32 devices: a whole 2x2x4 slice. The times are simulated.
32 devices in a mesh: pairs: 16 (over z, y, x), side: 2 (over core).
Axes of the slice: x: 2, y: 2, z: 4, core: 2. Of those that a mesh axis runs over, the one named last changes fastest.
Arguments:
- features: bfloat16 [16, 196, 768], P('pairs', None, 'side'), may hold values from -6 to 6
- image_slot: int32 [16], replicated, may hold values from 0 to 15, as said below
- slot_images: int32 [48, 2], P('pairs'), may hold values from 0 to 15, as said below
- slot_count: int32 [16], P('pairs'), may hold values from 1 to 3, as said below
- gain_self: float32 [2, 768], P('side'), may hold values from 0.5 to 1.5
- gain_query: float32 [2, 768], P('side'), may hold values from 0.5 to 1.5
- gain_memory: float32 [2, 768], P('side'), may hold values from 0.5 to 1.5
- gain_mlp: float32 [2, 768], P('side'), may hold values from 0.5 to 1.5
- gain_head: float32 [2, 768], P('side'), may hold values from 0.5 to 1.5
- w_qkv: bfloat16 [2, 768, 2304], P('side'), may hold values from -0.21875 to 0.21875
- w_self_out: bfloat16 [2, 768, 768], P('side'), may hold values from -0.21875 to 0.21875
- w_query: bfloat16 [2, 768, 768], P('side'), may hold values from -0.21875 to 0.21875
- w_memory: bfloat16 [2, 768, 1536], P('side'), may hold values from -0.21875 to 0.21875
- w_cross_out: bfloat16 [2, 768, 768], P('side'), may hold values from -0.21875 to 0.21875
- w_fc1: bfloat16 [2, 3072, 768], P('side', 'pairs'), may hold values from -0.21875 to 0.21875
- w_fc2: bfloat16 [2, 3072, 768], P('side', 'pairs'), may hold values from -0.109375 to 0.109375
- w_head: bfloat16 [2, 768, 1024], P('side'), may hold values from -0.21875 to 0.21875
Outputs:
- merged_points: bfloat16 [16, 196, 768], P('pairs', None, 'side')
Inputs may be any that keep to these rules, and one draw needn't show every extreme that they name: A permutation: image i is storage row image_slot[i] of features, held by device image_slot[i] // 1 of pairs. `slot_images`: slot j belongs to device j // 3 of pairs; its two images are distinct, and each is held by device (j // 3 + k) mod the size of pairs for some 0 <= k < 4; k = 3 occurs. `slot_count`: the counts sum to 32; 3 is reached on a quarter of the devices.
All inputs are finite; a program needn't handle non-finite values.
Results may differ from a plain program's by a relative error of at most 0.015.
Values may be sent and summed in bfloat16 or wider, within the bound.
A program may use at most 128 MiB of HBM per device.

v0:
```python
import functools

import jax
import jax.numpy as jnp
from jax import lax
from jax.experimental import pallas as pl
from jax.experimental.pallas import tpu as pltpu
from jax.sharding import PartitionSpec as P

HEAD_DIM = 64
WINDOW = 4
PAIR = 2 * HEAD_DIM
BLOCKS = 4
REACH = WINDOW + 1
VMEM_LIMIT = 63 * 1024 * 1024
MESH = pl.DeviceIdType.MESH


def padded(rows):
    return -(-rows // 16) * 16


def layer_norm(values, gain):
    center = values - jnp.mean(values, axis=-1, keepdims=True)
    spread = jnp.mean(center * center, axis=-1, keepdims=True)
    return center * lax.rsqrt(spread + 1e-06) * gain


def matmul(left, right):
    return jnp.dot(left, right, preferred_element_type=jnp.float32)


def matmul_t(left, right):
    return lax.dot_general(
        left, right, (((1,), (1,)), ((), ())), preferred_element_type=jnp.float32
    )


def attend(q_ref, k_ref, v_ref, k_at, v_at, o_ref, width, comm):
    rows = q_ref.shape[0]
    low = lax.broadcasted_iota(jnp.int32, (rows, PAIR), 1) < HEAD_DIM
    for pair in range(width // PAIR):
        if pair * PAIR == width // 2:
            comm()
        q = q_ref[:, pair * PAIR : (pair + 1) * PAIR]
        k = k_ref[:, k_at + pair * PAIR : k_at + (pair + 1) * PAIR]
        v = v_ref[:, v_at + pair * PAIR : v_at + (pair + 1) * PAIR]
        mixed = None
        for keep in (low, jnp.logical_not(low)):
            q_head = jnp.where(keep, q, jnp.zeros_like(q))
            v_head = jnp.where(keep, v, jnp.zeros_like(v))
            scores = matmul_t(q_head, k) * HEAD_DIM ** (-0.5)
            expon = jnp.exp(scores)
            weights = (expon / jnp.sum(expon, axis=-1, keepdims=True)).astype(jnp.bfloat16)
            part = matmul(weights, v_head)
            mixed = part if mixed is None else mixed + part
        o_ref[:, pair * PAIR : (pair + 1) * PAIR] = mixed.astype(jnp.bfloat16)


def remote(src, dst, send, recv, device):
    return pltpu.make_async_remote_copy(
        src_ref=src, dst_ref=dst, send_sem=send, recv_sem=recv, device_id=device,
        device_id_type=MESH,
    )


def decoder_kernel(
    image_slot, features, slot_images, slot_count,
    g_self, g_query, g_memory, g_mlp, g_head,
    w_qkv, w_self_out, w_query, w_memory, w_cross_out, w_fc1, w_fc2, w_head,
    out,
    win, table, counts, gains, m_qkv, m_self_out, m_query, m_memory, m_cross_out, m_head, ring_w,
    triple, kv, queries, mixed, second, hidden, raw, term, term_away, term_in, far_out, far_in,
    f_local, f_send, f_recv, fr_send, fr_recv, t_send, t_recv, g_send, g_recv, w_send, w_recv,
    s_send, r_send, r_recv, x_send, x_recv, a_send, a_recv, b_send, b_recv,
):
    devices = lax.axis_size("pairs")
    chips = devices // 2
    here = lax.axis_index("pairs")
    s = lax.axis_index("side")
    x = lax.rem(here, 2)
    q = lax.div(here, 2)
    rows = features.shape[1]
    width = m_qkv.shape[0]
    slots = second.shape[0]
    tall = second.shape[1]
    per = chips // BLOCKS
    shard = ring_w.shape[2]
    split = 2 if shard % 32 == 0 else 1
    kinds = 2 * split
    part = shard // split
    total_pieces = kinds * chips

    sibling = (here, 1 - s)
    partner = (2 * q + s, x)
    at_home = x == s

    def pair_of(step, flip):
        chip = lax.rem(q + (step + chips), chips)
        return 2 * chip + (1 - x if flip else x)

    up = jnp.where(
        lax.rem(q, 2) == 0,
        jnp.where(q + 2 < chips, q + 2, chips - 1),
        jnp.where(q >= 3, q - 2, 0),
    )
    down = jnp.where(
        lax.rem(q, 2) == 0,
        jnp.where(q == 0, 1, q - 2),
        jnp.where(q + 2 < chips, q + 2, chips - 2),
    )
    onward = (2 * jnp.where(s == 0, up, down) + x, s)

    mats = (
        (w_qkv, m_qkv), (w_self_out, m_self_out), (w_memory, m_memory), (w_query, m_query),
        (w_cross_out, m_cross_out),
    )
    half = w_head.shape[2] // 2
    weights = [(src.at[0], dst) for src, dst in mats]
    weights += [(w_head.at[0, :, h * half : (h + 1) * half], m_head.at[h]) for h in range(2)]
    gain_refs = (g_self, g_query, g_memory, g_mlp, g_head)
    fcs = (w_fc1, w_fc2)

    def slot_at(step, ring):
        return lax.div(step, per) * (2 * per) + ring * per + lax.rem(step, per)

    def ring_view(step, kind, ring):
        place = ring_w.at[lax.div(kind, split), slot_at(step, ring)]
        if split == 1:
            return place
        start = pl.multiple_of(lax.rem(kind, split) * part, part)
        return place.at[pl.ds(start, part)]

    def own_fc(kind):
        return fcs[kind // split].at[0, pl.ds((kind % split) * part, part)]

    own_win = pltpu.make_async_copy(features.at[0], win.at[x, s], f_local)
    own_win.start()

    @pl.when(at_home)
    def _():
        pltpu.make_async_copy(slot_images, table, t_recv.at[0]).start()
        pltpu.make_async_copy(slot_count, counts, t_recv.at[1]).start()
        for at, ref in enumerate(gain_refs):
            pltpu.make_async_copy(ref, gains.at[at], g_recv.at[at]).start()
        for kind in range(kinds):
            pltpu.make_async_copy(own_fc(kind), ring_view(0, kind, s), r_recv.at[0, kind]).start()
        for at, (src, dst) in enumerate(weights):
            pltpu.make_async_copy(src, dst, w_recv.at[at]).start()

    barrier = pltpu.get_barrier_semaphore()
    for step in range(-2, 3):
        for flip in range(2):
            if step or flip:
                pl.semaphore_signal(
                    barrier, inc=1, device_id=(pair_of(step, flip), s), device_id_type=MESH
                )
    pl.semaphore_signal(barrier, inc=1, device_id=sibling, device_id_type=MESH)

    @pl.when(jnp.logical_not(at_home))
    def _():
        pl.semaphore_signal(barrier, inc=1, device_id=partner, device_id_type=MESH)

    pl.semaphore_wait(barrier, 10 + (1 - at_home.astype(jnp.int32)))

    table_out = [
        remote(slot_images, table, t_send.at[0], t_recv.at[0], partner),
        remote(slot_count, counts, t_send.at[1], t_recv.at[1], partner),
    ]
    fc_out = [
        remote(own_fc(kind), ring_view(0, kind, x), s_send.at[kind], r_recv.at[0, kind], partner)
        for kind in range(kinds)
    ]
    gains_out = [
        remote(ref, gains.at[at], g_send.at[at], g_recv.at[at], sibling)
        for at, ref in enumerate(gain_refs)
    ]
    weights_out = [
        remote(src, dst, w_send.at[at], w_recv.at[at], sibling)
        for at, (src, dst) in enumerate(weights)
    ]

    def feature_out(step, flip):
        place = x + 2 * step
        return remote(
            features.at[0], win.at[place, s], f_send.at[2 * step + flip - 1], f_recv.at[place],
            (pair_of(-step, flip), s),
        )

    def relay(place):
        block = win.at[place, s]
        return remote(block, block, fr_send.at[place], fr_recv.at[place], sibling)

    @pl.when(jnp.logical_not(at_home))
    def _():
        for copy in table_out:
            copy.start()

    for step, flip in ((0, 1), (1, 0), (1, 1)):
        feature_out(step, flip).start()

    @pl.when(x == 0)
    def _():
        feature_out(2, 0).start()
        feature_out(2, 1).start()

    own_win.wait()
    relay(x).start()

    @pl.when(at_home)
    def _():
        for copy in gains_out:
            copy.start()
        weights_out[0].start()

    @pl.when(jnp.logical_not(at_home))
    def _():
        for copy in fc_out:
            copy.start()

    def piece(number):
        step, kind = lax.div(number, kinds), lax.rem(number, kinds)
        block = ring_view(step, kind, s)
        pltpu.make_async_copy(block, block, r_recv.at[step, kind]).wait()

        @pl.when(step < chips - 1)
        def _():
            remote(
                block, ring_view(step + 1, kind, s), r_send.at[step, kind],
                r_recv.at[step + 1, kind], onward,
            ).start()

        remote(block, block, x_send.at[step, kind], x_recv.at[step, kind], sibling).start()

    def pieces(low, high):
        def body(number, carry):
            piece(number)
            return carry

        lax.fori_loop(low, high, body, 0)

    pieces(0, kinds)

    @pl.when(at_home)
    def _():
        for copy in weights_out[1:]:
            copy.start()

    def arrived(place):
        block = win.at[place, s]
        pltpu.make_async_copy(block, block, f_recv.at[place]).wait()
        relay(place).start()

    arrived(1 - x)
    for place in range(2, REACH):
        arrived(place)
    early = 2 * kinds
    pieces(kinds, early)
    for place in range(REACH):
        block = win.at[place, 1 - s]
        pltpu.make_async_copy(block, block, fr_recv.at[place]).wait()
    pltpu.make_async_copy(slot_images, table, t_recv.at[0]).wait()
    pltpu.make_async_copy(slot_count, counts, t_recv.at[1]).wait()
    for at, ref in enumerate(gain_refs):
        pltpu.make_async_copy(ref, gains.at[at], g_recv.at[at]).wait()

    def weight_wait(at):
        src, dst = weights[at]
        pltpu.make_async_copy(src, dst, w_recv.at[at]).wait()

    def first_wait(slot, at):
        @pl.when(slot == 0)
        def _():
            weight_wait(at)

    def place_of(slot, column):
        stored = image_slot[table[slot, column]]
        ahead = lax.rem(stored - (2 * q + s) + devices, devices)
        return jnp.minimum(ahead, WINDOW - 1) + s

    def tokens_of(place):
        return jnp.concatenate([win[place, 0], win[place, 1]], axis=-1).astype(jnp.float32)

    stops = 6 * slots
    each = max((total_pieces * 26 // 32 - early) // stops, 0)
    fronted = early + each * stops

    def front(slot, carry):
        told = [0]

        def comm():
            base = early + (6 * slot + told[0]) * each
            told[0] += 1
            for at in range(each):
                piece(base + at)

        first_wait(slot, 0)
        tokens = tokens_of(place_of(slot, x))
        state = layer_norm(tokens, gains[0]).astype(jnp.bfloat16)
        triple[...] = matmul(state, m_qkv[...]).astype(jnp.bfloat16)
        comm()
        attend(triple, triple, triple, width, 2 * width, mixed, width, comm)
        first_wait(slot, 1)
        first = tokens + matmul(mixed[...], m_self_out[...])
        second[slot, 0:rows, :] = first
        comm()
        first_wait(slot, 2)
        first_wait(slot, 3)
        query_in = layer_norm(first, gains[1]).astype(jnp.bfloat16)
        memory = tokens_of(place_of(slot, 1 - x))
        memory_in = layer_norm(memory, gains[2]).astype(jnp.bfloat16)
        queries[...] = matmul(query_in, m_query[...]).astype(jnp.bfloat16)
        kv[...] = matmul(memory_in, m_memory[...]).astype(jnp.bfloat16)
        comm()
        attend(queries, kv, kv, 0, width, mixed, width, comm)
        first_wait(slot, 4)
        result = second[slot, 0:rows, :] + matmul(mixed[...], m_cross_out[...])
        second[slot, 0:rows, :] = result
        hidden[slot, 0:rows, :] = layer_norm(result, gains[3]).astype(jnp.bfloat16)
        comm()
        return carry

    second[...] = jnp.zeros_like(second)
    hidden[...] = jnp.zeros_like(hidden)
    lax.fori_loop(0, slots, front, 0)

    def relayed(block):
        def body(at, carry):
            step, kind = block * per + lax.div(at, kinds), lax.rem(at, kinds)
            view = ring_view(step, kind, 1 - s)
            pltpu.make_async_copy(view, view, x_recv.at[step, kind]).wait()
            return carry

        lax.fori_loop(0, per * kinds, body, 0)

    def expand(block, slot):
        wide = 2 * per * shard
        if shard % 16 == 0:
            fc1 = ring_w[0, pl.ds(block * 2 * per, 2 * per)].reshape(wide, width)
            fc2 = ring_w[1, pl.ds(block * 2 * per, 2 * per)].reshape(wide, width)
            groups = [(fc1, fc2)]
        else:
            groups = [
                (ring_w[0, block * 2 * per + at], ring_w[1, block * 2 * per + at])
                for at in range(2 * per)
            ]
        total = second[slot]
        for fc1, fc2 in groups:
            pre = matmul_t(hidden[slot], fc1)
            act = (pre * (1.0 + lax.erf(pre * 0.5**0.5)) * 0.5).astype(jnp.bfloat16)
            total = total + matmul(act, fc2)
        second[slot] = total

    left = total_pieces - fronted
    places = (BLOCKS - 1) * slots

    def expand_early(turn, carry):
        block, slot = lax.div(turn, slots), lax.rem(turn, slots)

        @pl.when(slot == 0)
        def _():
            relayed(block)

        expand(block, slot)
        pieces(fronted + lax.div(turn * left, places), fronted + lax.div((turn + 1) * left, places))
        return carry

    lax.fori_loop(0, places, expand_early, 0)
    relayed(BLOCKS - 1)

    def expand_last(slot, carry):
        expand(BLOCKS - 1, slot)
        hidden[slot] = layer_norm(second[slot], gains[4]).astype(jnp.bfloat16)
        return carry

    lax.fori_loop(0, slots, expand_last, 0)
    weight_wait(5)
    weight_wait(6)
    pix = half // 4

    def terms(which, target):
        for slot in range(slots):
            raw[slot] = matmul(hidden[slot], m_head[which])
        own = [place_of(slot, x) for slot in range(slots)]
        live = [slot < counts[0] for slot in range(slots)]
        for slot in range(slots):
            raw[slot, :, 3 * pix :] = 1.0 + jnp.exp(raw[slot, :, 3 * pix :])
        for comp in range(4):
            at = slice(comp * pix, (comp + 1) * pix)
            for place in range(REACH):
                sums = jnp.zeros((rows, pix), jnp.float32)
                for slot in range(slots):
                    conf = raw[slot, 0:rows, 3 * pix :]
                    value = conf if comp == 3 else conf * raw[slot, 0:rows, at]
                    chosen = jnp.logical_and(own[slot] == place, live[slot])
                    sums = sums + jnp.where(chosen, value, 0.0)
                target[place, :, at] = sums.astype(target.dtype)

    terms(1 - s, term_away)
    away = remote(term_away, term_in, a_send, a_recv, sibling)
    away.start()
    terms(s, term)
    away.wait_recv()

    def far_copy(place):
        step, to = place // 2, place % 2
        other = jnp.where(x == to, 0, 1)
        chip = lax.rem(q + step, chips)
        return remote(
            far_out.at[place], far_in.at[2 * step + other], b_send.at[place],
            b_recv.at[2 * step + other], (2 * chip + to, s),
        )

    for place in reversed(range(REACH)):
        joined = term[place] + term_in[place].astype(jnp.float32)
        if place < 2:
            term[place] = joined
        far_out[place] = joined.astype(jnp.bfloat16)
        if place < 2:

            @pl.when(x != place)
            def _(place=place):
                far_copy(place).start()

        else:
            far_copy(place).start()

    def far_wait(at):
        block = far_in.at[at]
        pltpu.make_async_copy(block, block, b_recv.at[at]).wait()

    total = term[x]
    for at in (1, 2, 3):
        far_wait(at)
        total = total + far_in[at].astype(jnp.float32)
    term[2] = total

    @pl.when(x == 0)
    def _():
        for at in (4, 5):
            far_wait(at)
        term[2] = term[2] + far_in[4].astype(jnp.float32) + far_in[5].astype(jnp.float32)

    conf = jnp.maximum(term[2, :, 3 * pix :], 1.0)
    for comp in range(3):
        at = slice(comp * pix, (comp + 1) * pix)
        out[0, :, at] = (term[2, :, at] / conf).astype(jnp.bfloat16)

    for step, flip in ((0, 1), (1, 0), (1, 1)):
        feature_out(step, flip).wait_send()

    @pl.when(x == 0)
    def _():
        feature_out(2, 0).wait_send()
        feature_out(2, 1).wait_send()

    for place in range(REACH):
        relay(place).wait_send()

    @pl.when(at_home)
    def _():
        for copy in gains_out + weights_out:
            copy.wait_send()

    @pl.when(jnp.logical_not(at_home))
    def _():
        for copy in table_out + fc_out:
            copy.wait_send()

    def drain(number, carry):
        step, kind = lax.div(number, kinds), lax.rem(number, kinds)
        block = ring_view(step, kind, s)

        @pl.when(step < chips - 1)
        def _():
            remote(
                block, block, r_send.at[step, kind], r_recv.at[step, kind], onward
            ).wait_send()

        remote(block, block, x_send.at[step, kind], x_recv.at[step, kind], sibling).wait_send()
        return carry

    lax.fori_loop(0, total_pieces, drain, 0)
    away.wait_send()
    for place in range(REACH):
        if place < 2:

            @pl.when(x != place)
            def _(place=place):
                far_copy(place).wait_send()

        else:
            far_copy(place).wait_send()


def on_device(
    features, image_slot, slot_images, slot_count, gain_self, gain_query, gain_memory, gain_mlp,
    gain_head, w_qkv, w_self_out, w_query, w_memory, w_cross_out, w_fc1, w_fc2, w_head,
):
    devices = lax.axis_size("pairs")
    chips = devices // 2
    blocks, rows, part = features.shape
    if blocks != 1 or chips % BLOCKS:
        raise ValueError("unsupported split")
    width = w_qkv.shape[1]
    slots = slot_images.shape[0]
    tall = padded(rows)
    shard = w_fc1.shape[1]
    kinds = 2 * (2 if shard % 32 == 0 else 1)
    half = w_head.shape[2] // 2
    bf16, f32 = jnp.bfloat16, jnp.float32
    dma = pltpu.SemaphoreType.DMA
    anywhere = pl.BlockSpec(memory_space=pl.ANY)
    return pl.pallas_call(
        decoder_kernel,
        out_shape=jax.ShapeDtypeStruct((1, rows, half * 3 // 4), bf16),
        in_specs=[pl.BlockSpec(memory_space=pltpu.SMEM)] + [anywhere] * 16,
        out_specs=pl.BlockSpec(memory_space=pltpu.VMEM),
        scratch_shapes=[
            pltpu.VMEM((REACH, 2, rows, part), bf16),
            pltpu.SMEM(slot_images.shape, jnp.int32),
            pltpu.SMEM(slot_count.shape, jnp.int32),
            pltpu.VMEM((5, 1, width), f32),
            pltpu.VMEM(w_qkv.shape[1:], bf16),
            pltpu.VMEM(w_self_out.shape[1:], bf16),
            pltpu.VMEM(w_query.shape[1:], bf16),
            pltpu.VMEM(w_memory.shape[1:], bf16),
            pltpu.VMEM(w_cross_out.shape[1:], bf16),
            pltpu.VMEM((2, width, half), bf16),
            pltpu.VMEM((2, devices, shard, width), bf16),
            pltpu.VMEM((rows, 3 * width), bf16),
            pltpu.VMEM((rows, 2 * width), bf16),
            pltpu.VMEM((rows, width), bf16),
            pltpu.VMEM((rows, width), bf16),
            pltpu.VMEM((slots, tall, width), f32),
            pltpu.VMEM((slots, tall, width), bf16),
            pltpu.VMEM((slots, tall, half), f32),
            pltpu.VMEM((REACH, rows, half), f32),
            pltpu.VMEM((REACH, rows, half), bf16),
            pltpu.VMEM((REACH, rows, half), bf16),
            pltpu.VMEM((REACH, rows, half), bf16),
            pltpu.VMEM((REACH + 1, rows, half), bf16),
            dma, dma((5,)), dma((REACH,)), dma((REACH,)), dma((REACH,)),
            dma((2,)), dma((2,)), dma((5,)), dma((5,)), dma((7,)), dma((7,)),
            dma((kinds,)), dma((chips, kinds)), dma((chips, kinds)), dma((chips, kinds)),
            dma((chips, kinds)), dma, dma, dma((REACH,)), dma((REACH + 1,)),
        ],
        compiler_params=pltpu.CompilerParams(
            collective_id=0, has_side_effects=True, vmem_limit_bytes=VMEM_LIMIT
        ),
    )(
        image_slot, features, slot_images, slot_count, gain_self, gain_query, gain_memory,
        gain_mlp, gain_head, w_qkv, w_self_out, w_query, w_memory, w_cross_out, w_fc1, w_fc2,
        w_head,
    )


def solution(mesh):
    placed = (
        P("pairs", None, "side"),
        P(),
        P("pairs", None),
        P("pairs"),
        P("side", None),
        P("side", None),
        P("side", None),
        P("side", None),
        P("side", None),
        P("side", None, None),
        P("side", None, None),
        P("side", None, None),
        P("side", None, None),
        P("side", None, None),
        P("side", "pairs", None),
        P("side", "pairs", None),
        P("side", None, None),
    )
    return jax.shard_map(
        on_device, mesh=mesh, in_specs=placed, out_specs=P("pairs", None, "side"), check_vma=False
    )
```

profile of v0, /device:TPU:0, one launch (start us, length us, event | category | flops | bytes accessed | tf_op | source)
XLA Modules:
  0.0 99.1 jit_solution(7218417857866267251)
XLA Ops:
  0.7 1.3 %copy.18.slot_images = s32[3,2]{1,0:T(4,128)} copy(s32[3,2]{0,1:T(2,128)} %param.19) | data formatting | bytes 48 | tf_op args[2]
  2.0 95.5 %shard_map.163 = bf16[1,196,384]{2,1,0:T(8,128)(2,1)} custom-call(s32[16]{0:T(128)} %image_slot.1, bf16[1,196,384]{2,1,0:T(8,128)(2,1)} %features.1, s32[3,2]{1,0:T(4,128)} %copy.18.slot_images, s32[1]{0:T(128)S(6)} %copy.20.slot_count, f32[1,768]{1,0:T(1,128)} %g_self.1, f32[1,768]{1,0:T(1,128)} %g_query.1, f32[1,768]{1,0:T(1,128)} %g_memory.1, ...), custom_call_target="tpu_custom_call" | custom-call | tf_op jit(solution)/shard_map/pallas_call | solution.py:514
  97.5 1.6 %copy.21 = bf16[1,196,384]{2,1,0:T(8,128)(2,1)} copy(bf16[1,196,384]{2,1,0:T(8,128)(2,1)} %shard_map.163) | data formatting | bytes 301056
where the time goes:
time: 99.2 us; the launch traced here: 99.1 us
  Pallas kernels  95.5 us (96%)
  local copies, waits for them, and re-layouts  2.93 us (3%)
    pallas_call x1, Pallas kernels, on_device(): pl.pallas_call(decoder_kernel, out_shape=jax.ShapeDtypeStruct((1, rows, h...  95.5 us
    unnamed x2, local copies, waits for them, and re-layouts  2.93 us

commit v1 on v0

--- a/solution.py
+++ b/solution.py
@@ -65,7 +65,7 @@
 
 
 def decoder_kernel(
-    image_slot, features, slot_images, slot_count,
+    image_slot, slot_images, slot_count, features,
     g_self, g_query, g_memory, g_mlp, g_head,
     w_qkv, w_self_out, w_query, w_memory, w_cross_out, w_fc1, w_fc2, w_head,
     out,
@@ -88,7 +88,7 @@
     shard = ring_w.shape[2]
     split = 2 if shard % 32 == 0 else 1
     kinds = 2 * split
-    part = shard // split
+    rank = shard // split
     total_pieces = kinds * chips
 
     sibling = (here, 1 - s)
@@ -125,26 +125,31 @@
         return lax.div(step, per) * (2 * per) + ring * per + lax.rem(step, per)
 
     def ring_view(step, kind, ring):
-        place = ring_w.at[lax.div(kind, split), slot_at(step, ring)]
+        place = ring_w.at[lax.rem(kind, 2), slot_at(step, ring)]
         if split == 1:
             return place
-        start = pl.multiple_of(lax.rem(kind, split) * part, part)
-        return place.at[pl.ds(start, part)]
-
-    def own_fc(kind):
-        return fcs[kind // split].at[0, pl.ds((kind % split) * part, part)]
+        return place.at[pl.ds(pl.multiple_of(lax.div(kind, 2) * rank, rank), rank)]
+
+    def own_fc(which, piece):
+        if split == 1:
+            return fcs[which].at[0]
+        return fcs[which].at[0, pl.ds(pl.multiple_of(piece * rank, rank), rank)]
 
     own_win = pltpu.make_async_copy(features.at[0], win.at[x, s], f_local)
     own_win.start()
 
     @pl.when(at_home)
     def _():
-        pltpu.make_async_copy(slot_images, table, t_recv.at[0]).start()
-        pltpu.make_async_copy(slot_count, counts, t_recv.at[1]).start()
+        for slot in range(slots):
+            for column in range(2):
+                table[slot, column] = slot_images[slot, column]
+        counts[0] = slot_count[0]
         for at, ref in enumerate(gain_refs):
             pltpu.make_async_copy(ref, gains.at[at], g_recv.at[at]).start()
-        for kind in range(kinds):
-            pltpu.make_async_copy(own_fc(kind), ring_view(0, kind, s), r_recv.at[0, kind]).start()
+        for which in range(2):
+            pltpu.make_async_copy(
+                own_fc(which, s), ring_view(0, which, s), r_recv.at[0, which]
+            ).start()
         for at, (src, dst) in enumerate(weights):
             pltpu.make_async_copy(src, dst, w_recv.at[at]).start()
 
@@ -167,10 +172,28 @@
         remote(slot_images, table, t_send.at[0], t_recv.at[0], partner),
         remote(slot_count, counts, t_send.at[1], t_recv.at[1], partner),
     ]
-    fc_out = [
-        remote(own_fc(kind), ring_view(0, kind, x), s_send.at[kind], r_recv.at[0, kind], partner)
-        for kind in range(kinds)
-    ]
+    across = (2 * q + s, s)
+    if split == 1:
+        fc_home = []
+        fc_out = [
+            remote(own_fc(f, 0), ring_view(0, f, x), s_send.at[f], r_recv.at[0, f], partner)
+            for f in range(2)
+        ]
+    else:
+        fc_home = [
+            remote(
+                own_fc(f, 1 - s), ring_view(0, f, 1 - s), s_send.at[f], r_recv.at[0, f], sibling
+            )
+            for f in range(2)
+        ]
+        fc_out = [
+            remote(
+                own_fc(f, ring), ring_view(0, 2 + f, ring), s_send.at[2 * f + to],
+                r_recv.at[0, 2 + f], device,
+            )
+            for f in range(2)
+            for to, (ring, device) in enumerate(((x, partner), (s, across)))
+        ]
     gains_out = [
         remote(ref, gains.at[at], g_send.at[at], g_recv.at[at], sibling)
         for at, ref in enumerate(gain_refs)
@@ -180,42 +203,43 @@
         for at, (src, dst) in enumerate(weights)
     ]
 
-    def feature_out(step, flip):
-        place = x + 2 * step
+    def feature_out(block, place, step, flip, at):
         return remote(
-            features.at[0], win.at[place, s], f_send.at[2 * step + flip - 1], f_recv.at[place],
-            (pair_of(-step, flip), s),
+            block, win.at[place, s], f_send.at[at], f_recv.at[place], (pair_of(-step, flip), s)
         )
 
-    def relay(place):
-        block = win.at[place, s]
-        return remote(block, block, fr_send.at[place], fr_recv.at[place], sibling)
-
-    @pl.when(jnp.logical_not(at_home))
-    def _():
-        for copy in table_out:
-            copy.start()
-
-    for step, flip in ((0, 1), (1, 0), (1, 1)):
-        feature_out(step, flip).start()
+    own = features.at[0]
+    passed = win.at[1 - x, s]
+    feature_first = [feature_out(own, x, 0, 1, 0), feature_out(own, x + 2, 1, 0, 1)]
+    feature_next = feature_out(passed, 3 - x, 1, 0, 2)
+    far_own = feature_out(own, WINDOW, 2, 0, 3)
+    far_passed = feature_out(passed, WINDOW, 2, 0, 3)
+
+    def relay(place, block=None):
+        target = win.at[place, s]
+        return remote(
+            target if block is None else block, target, fr_send.at[place], fr_recv.at[place],
+            sibling,
+        )
+
+    for copy in feature_first:
+        copy.start()
 
     @pl.when(x == 0)
     def _():
-        feature_out(2, 0).start()
-        feature_out(2, 1).start()
-
-    own_win.wait()
-    relay(x).start()
+        far_own.start()
+
+    relay(x, own).start()
 
     @pl.when(at_home)
     def _():
-        for copy in gains_out:
+        for copy in fc_home + gains_out:
             copy.start()
         weights_out[0].start()
 
     @pl.when(jnp.logical_not(at_home))
     def _():
-        for copy in fc_out:
+        for copy in table_out + fc_out:
             copy.start()
 
     def piece(number):
@@ -239,28 +263,41 @@
 
         lax.fori_loop(low, high, body, 0)
 
-    pieces(0, kinds)
-
-    @pl.when(at_home)
-    def _():
-        for copy in weights_out[1:]:
-            copy.start()
-
     def arrived(place):
         block = win.at[place, s]
         pltpu.make_async_copy(block, block, f_recv.at[place]).wait()
         relay(place).start()
 
+    pieces(0, kinds // 2)
     arrived(1 - x)
-    for place in range(2, REACH):
-        arrived(place)
+    feature_next.start()
+
+    @pl.when(x == 1)
+    def _():
+        far_passed.start()
+
+    arrived(2 + x)
+    pieces(kinds // 2, kinds)
+    arrived(3 - x)
+    arrived(4)
+
+    @pl.when(at_home)
+    def _():
+        for copy in weights_out[1:]:
+            copy.start()
+
     early = 2 * kinds
     pieces(kinds, early)
+    own_win.wait()
     for place in range(REACH):
         block = win.at[place, 1 - s]
         pltpu.make_async_copy(block, block, fr_recv.at[place]).wait()
-    pltpu.make_async_copy(slot_images, table, t_recv.at[0]).wait()
-    pltpu.make_async_copy(slot_count, counts, t_recv.at[1]).wait()
+
+    @pl.when(jnp.logical_not(at_home))
+    def _():
+        for copy in table_out:
+            copy.wait_recv()
+
     for at, ref in enumerate(gain_refs):
         pltpu.make_async_copy(ref, gains.at[at], g_recv.at[at]).wait()
 
@@ -446,20 +483,15 @@
         at = slice(comp * pix, (comp + 1) * pix)
         out[0, :, at] = (term[2, :, at] / conf).astype(jnp.bfloat16)
 
-    for step, flip in ((0, 1), (1, 0), (1, 1)):
-        feature_out(step, flip).wait_send()
-
-    @pl.when(x == 0)
-    def _():
-        feature_out(2, 0).wait_send()
-        feature_out(2, 1).wait_send()
+    for copy in feature_first + [feature_next, far_own]:
+        copy.wait_send()
 
     for place in range(REACH):
         relay(place).wait_send()
 
     @pl.when(at_home)
     def _():
-        for copy in gains_out + weights_out:
+        for copy in fc_home + gains_out + weights_out:
             copy.wait_send()
 
     @pl.when(jnp.logical_not(at_home))
@@ -514,7 +546,7 @@
     return pl.pallas_call(
         decoder_kernel,
         out_shape=jax.ShapeDtypeStruct((1, rows, half * 3 // 4), bf16),
-        in_specs=[pl.BlockSpec(memory_space=pltpu.SMEM)] + [anywhere] * 16,
+        in_specs=[pl.BlockSpec(memory_space=pltpu.SMEM)] * 3 + [anywhere] * 14,
         out_specs=pl.BlockSpec(memory_space=pltpu.VMEM),
         scratch_shapes=[
             pltpu.VMEM((REACH, 2, rows, part), bf16),
@@ -549,7 +581,7 @@
             collective_id=0, has_side_effects=True, vmem_limit_bytes=VMEM_LIMIT
         ),
     )(
-        image_slot, features, slot_images, slot_count, gain_self, gain_query, gain_memory,
+        image_slot, slot_images, slot_count, features, gain_self, gain_query, gain_memory,
         gain_mlp, gain_head, w_qkv, w_self_out, w_query, w_memory, w_cross_out, w_fc1, w_fc2,
         w_head,
     )

time: 99.2 us -> 96.4 us (0.972)
  Pallas kernels: 95.5 us -> 92.6 us
    pallas_call x1, Pallas kernels: 95.5 us -> 92.6 us  [on_device(): pl.pallas_call(decoder_kernel, out_shape=jax.ShapeDtypeStruct((1, rows, h...]
where the time goes in v1:
time: 96.4 us; the launch traced here: 96.2 us
  Pallas kernels  92.6 us (96%)
  local copies, waits for them, and re-layouts  2.93 us (3%)
    pallas_call x1, Pallas kernels, on_device(): pl.pallas_call(decoder_kernel, out_shape=jax.ShapeDtypeStruct((1, rows, h...  92.6 us
    unnamed x2, local copies, waits for them, and re-layouts  2.93 us

profile of v1, /device:TPU:0, one launch (start us, length us, event | category | flops | bytes accessed | tf_op | source)
XLA Modules:
  0.0 96.2 jit_solution(10795120266002213408)
XLA Ops:
  0.7 1.3 %copy.18.slot_images = s32[3,2]{1,0:T(4,128)} copy(s32[3,2]{0,1:T(2,128)} %param.19) | data formatting | bytes 48 | tf_op args[2]
  2.0 92.6 %shard_map.163 = bf16[1,196,384]{2,1,0:T(8,128)(2,1)} custom-call(s32[16]{0:T(128)} %image_slot.1, s32[3,2]{1,0:T(4,128)} %copy.18.slot_images, s32[1]{0:T(128)S(6)} %copy.20.slot_count, bf16[1,196,384]{2,1,0:T(8,128)(2,1)} %features.1, f32[1,768]{1,0:T(1,128)} %g_self.1, f32[1,768]{1,0:T(1,128)} %g_query.1, f32[1,768]{1,0:T(1,128)} %g_memory.1, ...), custom_call_target="tpu_custom_call" | custom-call | tf_op jit(solution)/shard_map/pallas_call | solution.py:546
  94.6 1.6 %copy.21 = bf16[1,196,384]{2,1,0:T(8,128)(2,1)} copy(bf16[1,196,384]{2,1,0:T(8,128)(2,1)} %shard_map.163) | data formatting | bytes 301056

commit v2 on v1

--- a/solution.py
+++ b/solution.py
@@ -71,6 +71,7 @@
     out,
     win, table, counts, gains, m_qkv, m_self_out, m_query, m_memory, m_cross_out, m_head, ring_w,
     triple, kv, queries, mixed, second, hidden, raw, term, term_away, term_in, far_out, far_in,
+    final,
     f_local, f_send, f_recv, fr_send, fr_recv, t_send, t_recv, g_send, g_recv, w_send, w_recv,
     s_send, r_send, r_recv, x_send, x_recv, a_send, a_recv, b_send, b_recv,
 ):
@@ -122,7 +123,7 @@
     fcs = (w_fc1, w_fc2)
 
     def slot_at(step, ring):
-        return lax.div(step, per) * (2 * per) + ring * per + lax.rem(step, per)
+        return 2 * step + ring
 
     def ring_view(step, kind, ring):
         place = ring_w.at[lax.rem(kind, 2), slot_at(step, ring)]
@@ -140,10 +141,6 @@
 
     @pl.when(at_home)
     def _():
-        for slot in range(slots):
-            for column in range(2):
-                table[slot, column] = slot_images[slot, column]
-        counts[0] = slot_count[0]
         for at, ref in enumerate(gain_refs):
             pltpu.make_async_copy(ref, gains.at[at], g_recv.at[at]).start()
         for which in range(2):
@@ -169,8 +166,8 @@
     pl.semaphore_wait(barrier, 10 + (1 - at_home.astype(jnp.int32)))
 
     table_out = [
-        remote(slot_images, table, t_send.at[0], t_recv.at[0], partner),
-        remote(slot_count, counts, t_send.at[1], t_recv.at[1], partner),
+        remote(slot_images, table, t_send.at[0], t_recv.at[0], (pair_of(0, 1), s)),
+        remote(slot_count, counts, t_send.at[1], t_recv.at[1], (pair_of(0, 1), s)),
     ]
     across = (2 * q + s, s)
     if split == 1:
@@ -210,10 +207,19 @@
 
     own = features.at[0]
     passed = win.at[1 - x, s]
-    feature_first = [feature_out(own, x, 0, 1, 0), feature_out(own, x + 2, 1, 0, 1)]
-    feature_next = feature_out(passed, 3 - x, 1, 0, 2)
-    far_own = feature_out(own, WINDOW, 2, 0, 3)
-    far_passed = feature_out(passed, WINDOW, 2, 0, 3)
+    even = lax.rem(q, 2) == 0
+    feature_across = feature_out(own, x, 0, 1, 0)
+    near_zero = [feature_out(block, 2, 1, 0, 1) for block in (own, passed)]
+    near_one = [feature_out(block, 3, 1, 0, 2) for block in (passed, own)]
+    far_zero = [feature_out(block, WINDOW, 2, 0, 3) for block in (own, passed)]
+    onto_next = feature_out(win.at[WINDOW, s], 2, -1, 0, 4)
+
+    def zero_start(at):
+        far_zero[at].start()
+
+        @pl.when(jnp.logical_not(even))
+        def _():
+            near_zero[at].start()
 
     def relay(place, block=None):
         target = win.at[place, s]
@@ -222,12 +228,17 @@
             sibling,
         )
 
-    for copy in feature_first:
+    for copy in table_out:
         copy.start()
+    feature_across.start()
 
     @pl.when(x == 0)
     def _():
-        far_own.start()
+        zero_start(0)
+
+    @pl.when(x == 1)
+    def _():
+        near_one[1].start()
 
     relay(x, own).start()
 
@@ -239,11 +250,19 @@
 
     @pl.when(jnp.logical_not(at_home))
     def _():
-        for copy in table_out + fc_out:
+        for copy in fc_out:
             copy.start()
 
     def piece(number):
-        step, kind = lax.div(number, kinds), lax.rem(number, kinds)
+        turn = lax.div(number, kinds // 2)
+        last = turn == 2 * chips - 1
+        ahead = jnp.logical_or(turn == 0, jnp.logical_and(lax.rem(turn, 2) == 1, turn < 2 * chips - 1))
+        step = jnp.where(
+            turn == 0,
+            0,
+            jnp.where(last, chips - 1, jnp.where(ahead, lax.div(turn + 1, 2), lax.div(turn, 2) - 1)),
+        )
+        kind = lax.rem(number, kinds // 2) + jnp.where(ahead, 0, kinds // 2)
         block = ring_view(step, kind, s)
         pltpu.make_async_copy(block, block, r_recv.at[step, kind]).wait()
 
@@ -268,36 +287,48 @@
         pltpu.make_async_copy(block, block, f_recv.at[place]).wait()
         relay(place).start()
 
-    pieces(0, kinds // 2)
+    group = kinds // 2
+    early = 4 * group
+    pieces(0, group)
     arrived(1 - x)
-    feature_next.start()
+
+    @pl.when(x == 0)
+    def _():
+        near_one[0].start()
 
     @pl.when(x == 1)
     def _():
-        far_passed.start()
-
-    arrived(2 + x)
-    pieces(kinds // 2, kinds)
-    arrived(3 - x)
-    arrived(4)
+        zero_start(1)
+
+    pieces(group, 2 * group)
+    arrived(WINDOW)
+
+    @pl.when(even)
+    def _():
+        onto_next.start()
+
+    arrived(3)
+    pieces(2 * group, 3 * group)
 
     @pl.when(at_home)
     def _():
-        for copy in weights_out[1:]:
+        for copy in weights_out[1:2]:
             copy.start()
 
-    early = 2 * kinds
-    pieces(kinds, early)
+    pieces(3 * group, early)
+    arrived(2)
+
+    @pl.when(at_home)
+    def _():
+        for copy in weights_out[2:]:
+            copy.start()
+
     own_win.wait()
     for place in range(REACH):
         block = win.at[place, 1 - s]
         pltpu.make_async_copy(block, block, fr_recv.at[place]).wait()
-
-    @pl.when(jnp.logical_not(at_home))
-    def _():
-        for copy in table_out:
-            copy.wait_recv()
-
+    for copy in table_out:
+        copy.wait_recv()
     for at, ref in enumerate(gain_refs):
         pltpu.make_async_copy(ref, gains.at[at], g_recv.at[at]).wait()
 
@@ -310,10 +341,15 @@
         def _():
             weight_wait(at)
 
-    def place_of(slot, column):
-        stored = image_slot[table[slot, column]]
-        ahead = lax.rem(stored - (2 * q + s) + devices, devices)
-        return jnp.minimum(ahead, WINDOW - 1) + s
+    def entry(slot, column, core):
+        local = slot_images[slot, column]
+        return jnp.where(x == core, local, table[slot, column])
+
+    def place_of(slot, column, core=None):
+        core = s if core is None else core
+        stored = image_slot[entry(slot, column, core)]
+        ahead = lax.rem(stored - (2 * q + core) + devices, devices)
+        return jnp.minimum(ahead, WINDOW - 1) + core
 
     def tokens_of(place):
         return jnp.concatenate([win[place, 0], win[place, 1]], axis=-1).astype(jnp.float32)
@@ -361,26 +397,23 @@
     hidden[...] = jnp.zeros_like(hidden)
     lax.fori_loop(0, slots, front, 0)
 
-    def relayed(block):
+    def relayed(first, steps):
         def body(at, carry):
-            step, kind = block * per + lax.div(at, kinds), lax.rem(at, kinds)
+            step, kind = first + lax.div(at, kinds), lax.rem(at, kinds)
             view = ring_view(step, kind, 1 - s)
             pltpu.make_async_copy(view, view, x_recv.at[step, kind]).wait()
             return carry
 
-        lax.fori_loop(0, per * kinds, body, 0)
-
-    def expand(block, slot):
-        wide = 2 * per * shard
+        lax.fori_loop(0, steps * kinds, body, 0)
+
+    def expand(first, steps, slot):
+        count = 2 * steps
         if shard % 16 == 0:
-            fc1 = ring_w[0, pl.ds(block * 2 * per, 2 * per)].reshape(wide, width)
-            fc2 = ring_w[1, pl.ds(block * 2 * per, 2 * per)].reshape(wide, width)
-            groups = [(fc1, fc2)]
+            groups = [
+                [ring_w[f, pl.ds(2 * first, count)].reshape(count * shard, width) for f in range(2)]
+            ]
         else:
-            groups = [
-                (ring_w[0, block * 2 * per + at], ring_w[1, block * 2 * per + at])
-                for at in range(2 * per)
-            ]
+            groups = [[ring_w[f, 2 * first + at] for f in range(2)] for at in range(count)]
         total = second[slot]
         for fc1, fc2 in groups:
             pre = matmul_t(hidden[slot], fc1)
@@ -388,7 +421,8 @@
             total = total + matmul(act, fc2)
         second[slot] = total
 
-    left = total_pieces - fronted
+    whole = total_pieces - group
+    left = whole - fronted
     places = (BLOCKS - 1) * slots
 
     def expand_early(turn, carry):
@@ -396,48 +430,69 @@
 
         @pl.when(slot == 0)
         def _():
-            relayed(block)
-
-        expand(block, slot)
+            relayed(block * per, per)
+
+        expand(block * per, per, slot)
         pieces(fronted + lax.div(turn * left, places), fronted + lax.div((turn + 1) * left, places))
         return carry
 
     lax.fori_loop(0, places, expand_early, 0)
-    relayed(BLOCKS - 1)
-
-    def expand_last(slot, carry):
-        expand(BLOCKS - 1, slot)
-        hidden[slot] = layer_norm(second[slot], gains[4]).astype(jnp.bfloat16)
+    relayed((BLOCKS - 1) * per, per - 1)
+
+    def expand_late(slot, carry):
+        expand((BLOCKS - 1) * per, per - 1, slot)
+        pieces(
+            whole + lax.div(slot * group, slots), whole + lax.div((slot + 1) * group, slots)
+        )
         return carry
 
-    lax.fori_loop(0, slots, expand_last, 0)
+    lax.fori_loop(0, slots, expand_late, 0)
     weight_wait(5)
     weight_wait(6)
+    relayed(chips - 1, 1)
     pix = half // 4
 
-    def terms(which, target):
-        for slot in range(slots):
-            raw[slot] = matmul(hidden[slot], m_head[which])
-        own = [place_of(slot, x) for slot in range(slots)]
-        live = [slot < counts[0] for slot in range(slots)]
-        for slot in range(slots):
-            raw[slot, :, 3 * pix :] = 1.0 + jnp.exp(raw[slot, :, 3 * pix :])
+    def terms(slot, which, target):
+        raw[...] = matmul(hidden[slot], m_head[which])
+        conf = 1.0 + jnp.exp(raw[0:rows, 3 * pix :])
         for comp in range(4):
             at = slice(comp * pix, (comp + 1) * pix)
-            for place in range(REACH):
-                sums = jnp.zeros((rows, pix), jnp.float32)
-                for slot in range(slots):
-                    conf = raw[slot, 0:rows, 3 * pix :]
-                    value = conf if comp == 3 else conf * raw[slot, 0:rows, at]
-                    chosen = jnp.logical_and(own[slot] == place, live[slot])
-                    sums = sums + jnp.where(chosen, value, 0.0)
-                target[place, :, at] = sums.astype(target.dtype)
-
-    terms(1 - s, term_away)
-    away = remote(term_away, term_in, a_send, a_recv, sibling)
-    away.start()
-    terms(s, term)
-    away.wait_recv()
+            value = conf if comp == 3 else conf * raw[0:rows, at]
+            target[slot, :, at] = value.astype(target.dtype)
+
+    def away(slot):
+        return remote(
+            term_away.at[slot], term_in.at[slot], a_send.at[slot], a_recv.at[slot], sibling
+        )
+
+    def expand_last(slot, carry):
+        expand(chips - 1, 1, slot)
+        hidden[slot] = layer_norm(second[slot], gains[4]).astype(jnp.bfloat16)
+        terms(slot, 1 - s, term_away)
+        away(slot).start()
+        return carry
+
+    def own_terms(slot, carry):
+        terms(slot, s, term)
+        return carry
+
+    lax.fori_loop(0, slots, expand_last, 0)
+    lax.fori_loop(0, slots, own_terms, 0)
+    for slot in range(slots):
+        away(slot).wait_recv()
+
+    sources = []
+    for core, ref in ((s, term), (1 - s, term_in)):
+        live = jnp.where(x == core, slot_count[0], counts[0])
+        for slot in range(slots):
+            sources.append((place_of(slot, x, core), slot < live, ref, slot))
+
+    def sums_of(place):
+        sums = jnp.zeros((rows, half), jnp.float32)
+        for to, live, ref, slot in sources:
+            chosen = jnp.logical_and(to == place, live)
+            sums = sums + jnp.where(chosen, ref[slot].astype(jnp.float32), 0.0)
+        return sums
 
     def far_copy(place):
         step, to = place // 2, place % 2
@@ -448,43 +503,48 @@
             b_recv.at[2 * step + other], (2 * chip + to, s),
         )
 
-    for place in reversed(range(REACH)):
-        joined = term[place] + term_in[place].astype(jnp.float32)
-        if place < 2:
-            term[place] = joined
-        far_out[place] = joined.astype(jnp.bfloat16)
-        if place < 2:
-
-            @pl.when(x != place)
-            def _(place=place):
-                far_copy(place).start()
-
-        else:
+    for place in reversed(range(2, REACH)):
+        far_out[place] = sums_of(place).astype(jnp.bfloat16)
+        far_copy(place).start()
+    far_out[1 - x] = sums_of(1 - x).astype(jnp.bfloat16)
+    for place in range(2):
+
+        @pl.when(x != place)
+        def _(place=place):
             far_copy(place).start()
+
+    total = sums_of(x)
 
     def far_wait(at):
         block = far_in.at[at]
         pltpu.make_async_copy(block, block, b_recv.at[at]).wait()
 
-    total = term[x]
     for at in (1, 2, 3):
         far_wait(at)
         total = total + far_in[at].astype(jnp.float32)
-    term[2] = total
+    final[...] = total
 
     @pl.when(x == 0)
     def _():
         for at in (4, 5):
             far_wait(at)
-        term[2] = term[2] + far_in[4].astype(jnp.float32) + far_in[5].astype(jnp.float32)
-
-    conf = jnp.maximum(term[2, :, 3 * pix :], 1.0)
+        final[...] = final[...] + far_in[4].astype(jnp.float32) + far_in[5].astype(jnp.float32)
+
+    conf = jnp.maximum(final[:, 3 * pix :], 1.0)
     for comp in range(3):
         at = slice(comp * pix, (comp + 1) * pix)
-        out[0, :, at] = (term[2, :, at] / conf).astype(jnp.bfloat16)
-
-    for copy in feature_first + [feature_next, far_own]:
+        out[0, :, at] = (final[:, at] / conf).astype(jnp.bfloat16)
+
+    for copy in (feature_across, near_one[0], far_zero[0]):
         copy.wait_send()
+
+    @pl.when(even)
+    def _():
+        onto_next.wait_send()
+
+    @pl.when(jnp.logical_not(even))
+    def _():
+        near_zero[0].wait_send()
 
     for place in range(REACH):
         relay(place).wait_send()
@@ -496,8 +556,11 @@
 
     @pl.when(jnp.logical_not(at_home))
     def _():
-        for copy in table_out + fc_out:
+        for copy in fc_out:
             copy.wait_send()
+
+    for copy in table_out:
+        copy.wait_send()
 
     def drain(number, carry):
         step, kind = lax.div(number, kinds), lax.rem(number, kinds)
@@ -513,7 +576,8 @@
         return carry
 
     lax.fori_loop(0, total_pieces, drain, 0)
-    away.wait_send()
+    for slot in range(slots):
+        away(slot).wait_send()
     for place in range(REACH):
         if place < 2:
 
@@ -566,16 +630,17 @@
             pltpu.VMEM((rows, width), bf16),
             pltpu.VMEM((slots, tall, width), f32),
             pltpu.VMEM((slots, tall, width), bf16),
-            pltpu.VMEM((slots, tall, half), f32),
-            pltpu.VMEM((REACH, rows, half), f32),
-            pltpu.VMEM((REACH, rows, half), bf16),
-            pltpu.VMEM((REACH, rows, half), bf16),
+            pltpu.VMEM((tall, half), f32),
+            pltpu.VMEM((slots, rows, half), f32),
+            pltpu.VMEM((slots, rows, half), bf16),
+            pltpu.VMEM((slots, rows, half), bf16),
             pltpu.VMEM((REACH, rows, half), bf16),
             pltpu.VMEM((REACH + 1, rows, half), bf16),
+            pltpu.VMEM((rows, half), f32),
             dma, dma((5,)), dma((REACH,)), dma((REACH,)), dma((REACH,)),
             dma((2,)), dma((2,)), dma((5,)), dma((5,)), dma((7,)), dma((7,)),
             dma((kinds,)), dma((chips, kinds)), dma((chips, kinds)), dma((chips, kinds)),
-            dma((chips, kinds)), dma, dma, dma((REACH,)), dma((REACH + 1,)),
+            dma((chips, kinds)), dma((slots,)), dma((slots,)), dma((REACH,)), dma((REACH + 1,)),
         ],
         compiler_params=pltpu.CompilerParams(
             collective_id=0, has_side_effects=True, vmem_limit_bytes=VMEM_LIMIT

time: 96.4 us -> 99.9 us (1.036)
  Pallas kernels: 92.6 us -> 96.1 us
    pallas_call x1, Pallas kernels: 92.6 us -> 96.1 us  [on_device(): pl.pallas_call(decoder_kernel, out_shape=jax.ShapeDtypeStruct((1, rows, h...]
where the time goes in v2:
time: 99.9 us; the launch traced here: 99.7 us
  Pallas kernels  96.1 us (96%)
  local copies, waits for them, and re-layouts  2.93 us (3%)
    pallas_call x1, Pallas kernels, on_device(): pl.pallas_call(decoder_kernel, out_shape=jax.ShapeDtypeStruct((1, rows, h...  96.1 us
    unnamed x2, local copies, waits for them, and re-layouts  2.93 us

profile of v2, /device:TPU:0, one launch (start us, length us, event | category | flops | bytes accessed | tf_op | source)
XLA Modules:
  0.0 99.7 jit_solution(17441023786126103577)
XLA Ops:
  0.7 1.3 %copy.18.slot_images = s32[3,2]{1,0:T(4,128)} copy(s32[3,2]{0,1:T(2,128)} %param.19) | data formatting | bytes 48 | tf_op args[2]
  2.0 96.1 %shard_map.163 = bf16[1,196,384]{2,1,0:T(8,128)(2,1)} custom-call(s32[16]{0:T(128)} %image_slot.1, s32[3,2]{1,0:T(4,128)} %copy.18.slot_images, s32[1]{0:T(128)S(6)} %copy.20.slot_count, bf16[1,196,384]{2,1,0:T(8,128)(2,1)} %features.1, f32[1,768]{1,0:T(1,128)} %g_self.1, f32[1,768]{1,0:T(1,128)} %g_query.1, f32[1,768]{1,0:T(1,128)} %g_memory.1, ...), custom_call_target="tpu_custom_call" | custom-call | tf_op jit(solution)/shard_map/pallas_call | solution.py:610
  98.1 1.6 %copy.21 = bf16[1,196,384]{2,1,0:T(8,128)(2,1)} copy(bf16[1,196,384]{2,1,0:T(8,128)(2,1)} %shard_map.163) | data formatting | bytes 301056

commit v3 on v2

--- a/solution.py
+++ b/solution.py
@@ -208,18 +208,13 @@
     own = features.at[0]
     passed = win.at[1 - x, s]
     even = lax.rem(q, 2) == 0
+    near, far = 2 + x, WINDOW
     feature_across = feature_out(own, x, 0, 1, 0)
-    near_zero = [feature_out(block, 2, 1, 0, 1) for block in (own, passed)]
-    near_one = [feature_out(block, 3, 1, 0, 2) for block in (passed, own)]
-    far_zero = [feature_out(block, WINDOW, 2, 0, 3) for block in (own, passed)]
-    onto_next = feature_out(win.at[WINDOW, s], 2, -1, 0, 4)
-
-    def zero_start(at):
-        far_zero[at].start()
-
-        @pl.when(jnp.logical_not(even))
-        def _():
-            near_zero[at].start()
+    feature_near = feature_out(own, near, 1, 0, 1)
+    feature_far = feature_out(own, far, 2, 0, 2)
+    feature_onto = feature_out(win.at[far, s], 2, -1, 0, 3)
+    near_across = feature_out(win.at[near, s], near, 0, 1, 4)
+    far_across = feature_out(win.at[far, s], far, 0, 1, 5)
 
     def relay(place, block=None):
         target = win.at[place, s]
@@ -232,13 +227,15 @@
         copy.start()
     feature_across.start()
 
+    by_near = jnp.logical_or(x == 1, jnp.logical_not(even))
+
     @pl.when(x == 0)
     def _():
-        zero_start(0)
-
-    @pl.when(x == 1)
-    def _():
-        near_one[1].start()
+        feature_far.start()
+
+    @pl.when(by_near)
+    def _():
+        feature_near.start()
 
     relay(x, own).start()
 
@@ -291,23 +288,19 @@
     early = 4 * group
     pieces(0, group)
     arrived(1 - x)
+    pieces(group, 2 * group)
 
     @pl.when(x == 0)
     def _():
-        near_one[0].start()
-
-    @pl.when(x == 1)
-    def _():
-        zero_start(1)
-
-    pieces(group, 2 * group)
-    arrived(WINDOW)
-
-    @pl.when(even)
-    def _():
-        onto_next.start()
-
-    arrived(3)
+        arrived(far)
+        far_across.start()
+
+        @pl.when(even)
+        def _():
+            feature_onto.start()
+
+    arrived(near)
+    near_across.start()
     pieces(2 * group, 3 * group)
 
     @pl.when(at_home)
@@ -315,8 +308,13 @@
         for copy in weights_out[1:2]:
             copy.start()
 
+    arrived(3 - x)
+
+    @pl.when(x == 1)
+    def _():
+        arrived(far)
+
     pieces(3 * group, early)
-    arrived(2)
 
     @pl.when(at_home)
     def _():
@@ -424,6 +422,7 @@
     whole = total_pieces - group
     left = whole - fronted
     places = (BLOCKS - 1) * slots
+    rate = -(-left // BLOCKS)
 
     def expand_early(turn, carry):
         block, slot = lax.div(turn, slots), lax.rem(turn, slots)
@@ -433,7 +432,9 @@
             relayed(block * per, per)
 
         expand(block * per, per, slot)
-        pieces(fronted + lax.div(turn * left, places), fronted + lax.div((turn + 1) * left, places))
+        pieces(
+            fronted + jnp.minimum(turn * rate, left), fronted + jnp.minimum((turn + 1) * rate, left)
+        )
         return carry
 
     lax.fori_loop(0, places, expand_early, 0)
@@ -535,16 +536,21 @@
         at = slice(comp * pix, (comp + 1) * pix)
         out[0, :, at] = (final[:, at] / conf).astype(jnp.bfloat16)
 
-    for copy in (feature_across, near_one[0], far_zero[0]):
+    for copy in (feature_across, near_across):
         copy.wait_send()
 
-    @pl.when(even)
-    def _():
-        onto_next.wait_send()
-
-    @pl.when(jnp.logical_not(even))
-    def _():
-        near_zero[0].wait_send()
+    @pl.when(x == 0)
+    def _():
+        feature_far.wait_send()
+        far_across.wait_send()
+
+        @pl.when(even)
+        def _():
+            feature_onto.wait_send()
+
+    @pl.when(by_near)
+    def _():
+        feature_near.wait_send()
 
     for place in range(REACH):
         relay(place).wait_send()
@@ -637,7 +643,7 @@
             pltpu.VMEM((REACH, rows, half), bf16),
             pltpu.VMEM((REACH + 1, rows, half), bf16),
             pltpu.VMEM((rows, half), f32),
-            dma, dma((5,)), dma((REACH,)), dma((REACH,)), dma((REACH,)),
+            dma, dma((6,)), dma((REACH,)), dma((REACH,)), dma((REACH,)),
             dma((2,)), dma((2,)), dma((5,)), dma((5,)), dma((7,)), dma((7,)),
             dma((kinds,)), dma((chips, kinds)), dma((chips, kinds)), dma((chips, kinds)),
             dma((chips, kinds)), dma((slots,)), dma((slots,)), dma((REACH,)), dma((REACH + 1,)),

time: 99.9 us -> 100 us (level)
  no operation moved by 1% of the time
where the time goes in v3:
time: 100 us; the launch traced here: 99.8 us
  Pallas kernels  96.2 us (96%)
  local copies, waits for them, and re-layouts  2.93 us (3%)
    pallas_call x1, Pallas kernels, on_device(): pl.pallas_call(decoder_kernel, out_shape=jax.ShapeDtypeStruct((1, rows, h...  96.2 us
    unnamed x2, local copies, waits for them, and re-layouts  2.93 us

profile of v3, /device:TPU:0, one launch (start us, length us, event | category | flops | bytes accessed | tf_op | source)
XLA Modules:
  0.0 99.8 jit_solution(17519194426485858425)
XLA Ops:
  0.7 1.3 %copy.18.slot_images = s32[3,2]{1,0:T(4,128)} copy(s32[3,2]{0,1:T(2,128)} %param.19) | data formatting | bytes 48 | tf_op args[2]
  2.0 96.2 %shard_map.163 = bf16[1,196,384]{2,1,0:T(8,128)(2,1)} custom-call(s32[16]{0:T(128)} %image_slot.1, s32[3,2]{1,0:T(4,128)} %copy.18.slot_images, s32[1]{0:T(128)S(6)} %copy.20.slot_count, bf16[1,196,384]{2,1,0:T(8,128)(2,1)} %features.1, f32[1,768]{1,0:T(1,128)} %g_self.1, f32[1,768]{1,0:T(1,128)} %g_query.1, f32[1,768]{1,0:T(1,128)} %g_memory.1, ...), custom_call_target="tpu_custom_call" | custom-call | tf_op jit(solution)/shard_map/pallas_call | solution.py:616
  98.2 1.6 %copy.21 = bf16[1,196,384]{2,1,0:T(8,128)(2,1)} copy(bf16[1,196,384]{2,1,0:T(8,128)(2,1)} %shard_map.163) | data formatting | bytes 301056

commit v4 on v2

--- a/solution.py
+++ b/solution.py
@@ -288,7 +288,7 @@
         relay(place).start()
 
     group = kinds // 2
-    early = 4 * group
+    early = 3 * group
     pieces(0, group)
     arrived(1 - x)
 
@@ -300,29 +300,22 @@
     def _():
         zero_start(1)
 
+    arrived(WINDOW)
+
+    @pl.when(even)
+    def _():
+        onto_next.start()
+
     pieces(group, 2 * group)
-    arrived(WINDOW)
-
-    @pl.when(even)
-    def _():
-        onto_next.start()
-
     arrived(3)
-    pieces(2 * group, 3 * group)
+    arrived(2)
 
     @pl.when(at_home)
     def _():
-        for copy in weights_out[1:2]:
+        for copy in weights_out[1:]:
             copy.start()
 
-    pieces(3 * group, early)
-    arrived(2)
-
-    @pl.when(at_home)
-    def _():
-        for copy in weights_out[2:]:
-            copy.start()
-
+    pieces(2 * group, early)
     own_win.wait()
     for place in range(REACH):
         block = win.at[place, 1 - s]
@@ -424,6 +417,7 @@
     whole = total_pieces - group
     left = whole - fronted
     places = (BLOCKS - 1) * slots
+    rate = -(-left // (2 * slots))
 
     def expand_early(turn, carry):
         block, slot = lax.div(turn, slots), lax.rem(turn, slots)
@@ -433,7 +427,9 @@
             relayed(block * per, per)
 
         expand(block * per, per, slot)
-        pieces(fronted + lax.div(turn * left, places), fronted + lax.div((turn + 1) * left, places))
+        pieces(
+            fronted + jnp.minimum(turn * rate, left), fronted + jnp.minimum((turn + 1) * rate, left)
+        )
         return carry
 
     lax.fori_loop(0, places, expand_early, 0)
@@ -494,42 +490,41 @@
             sums = sums + jnp.where(chosen, ref[slot].astype(jnp.float32), 0.0)
         return sums
 
-    def far_copy(place):
-        step, to = place // 2, place % 2
-        other = jnp.where(x == to, 0, 1)
-        chip = lax.rem(q + step, chips)
+    def far_copy(at, step, flip):
         return remote(
-            far_out.at[place], far_in.at[2 * step + other], b_send.at[place],
-            b_recv.at[2 * step + other], (2 * chip + to, s),
+            far_out.at[at], far_in.at[at], b_send.at[at], b_recv.at[at], (pair_of(step, flip), s)
         )
 
-    for place in reversed(range(2, REACH)):
-        far_out[place] = sums_of(place).astype(jnp.bfloat16)
-        far_copy(place).start()
-    far_out[1 - x] = sums_of(1 - x).astype(jnp.bfloat16)
-    for place in range(2):
-
-        @pl.when(x != place)
-        def _(place=place):
-            far_copy(place).start()
-
-    total = sums_of(x)
+    def far_send(at, step, flip, sums):
+        far_out[at] = sums.astype(jnp.bfloat16)
+        far_copy(at, step, flip).start()
 
     def far_wait(at):
         block = far_in.at[at]
         pltpu.make_async_copy(block, block, b_recv.at[at]).wait()
-
-    for at in (1, 2, 3):
-        far_wait(at)
-        total = total + far_in[at].astype(jnp.float32)
-    final[...] = total
+        return block[...].astype(jnp.float32)
+
+    far_send(0, 2, 0, sums_of(WINDOW))
+    far_send(1, 0, 1, sums_of(3 - x))
 
     @pl.when(x == 0)
     def _():
-        for at in (4, 5):
-            far_wait(at)
-        final[...] = final[...] + far_in[4].astype(jnp.float32) + far_in[5].astype(jnp.float32)
-
+        far_send(3, 0, 1, sums_of(1))
+
+    final[...] = sums_of(2 + x)
+    far_send(2, 1, 0, final[...] + far_wait(1))
+    final[...] = sums_of(x)
+
+    @pl.when(x == 1)
+    def _():
+        far_send(3, 0, 1, sums_of(0) + far_wait(0))
+
+    @pl.when(x == 0)
+    def _():
+        final[...] = final[...] + far_wait(0)
+
+    final[...] = final[...] + far_wait(2)
+    final[...] = final[...] + far_wait(3)
     conf = jnp.maximum(final[:, 3 * pix :], 1.0)
     for comp in range(3):
         at = slice(comp * pix, (comp + 1) * pix)
@@ -578,15 +573,8 @@
     lax.fori_loop(0, total_pieces, drain, 0)
     for slot in range(slots):
         away(slot).wait_send()
-    for place in range(REACH):
-        if place < 2:
-
-            @pl.when(x != place)
-            def _(place=place):
-                far_copy(place).wait_send()
-
-        else:
-            far_copy(place).wait_send()
+    for at, (step, flip) in enumerate(((2, 0), (0, 1), (1, 0), (0, 1))):
+        far_copy(at, step, flip).wait_send()
 
 
 def on_device(
@@ -634,13 +622,13 @@
             pltpu.VMEM((slots, rows, half), f32),
             pltpu.VMEM((slots, rows, half), bf16),
             pltpu.VMEM((slots, rows, half), bf16),
-            pltpu.VMEM((REACH, rows, half), bf16),
-            pltpu.VMEM((REACH + 1, rows, half), bf16),
+            pltpu.VMEM((4, rows, half), bf16),
+            pltpu.VMEM((4, rows, half), bf16),
             pltpu.VMEM((rows, half), f32),
             dma, dma((5,)), dma((REACH,)), dma((REACH,)), dma((REACH,)),
             dma((2,)), dma((2,)), dma((5,)), dma((5,)), dma((7,)), dma((7,)),
             dma((kinds,)), dma((chips, kinds)), dma((chips, kinds)), dma((chips, kinds)),
-            dma((chips, kinds)), dma((slots,)), dma((slots,)), dma((REACH,)), dma((REACH + 1,)),
+            dma((chips, kinds)), dma((slots,)), dma((slots,)), dma((4,)), dma((4,)),
         ],
         compiler_params=pltpu.CompilerParams(
             collective_id=0, has_side_effects=True, vmem_limit_bytes=VMEM_LIMIT

time: 99.9 us -> 93.4 us (0.935)
  Pallas kernels: 96.1 us -> 89.7 us
    pallas_call x1, Pallas kernels: 96.1 us -> 89.7 us  [on_device(): pl.pallas_call(decoder_kernel, out_shape=jax.ShapeDtypeStruct((1, rows, h...]
where the time goes in v4:
time: 93.4 us; the launch traced here: 93.2 us
  Pallas kernels  89.7 us (96%)
  local copies, waits for them, and re-layouts  2.93 us (3%)
    pallas_call x1, Pallas kernels, on_device(): pl.pallas_call(decoder_kernel, out_shape=jax.ShapeDtypeStruct((1, rows, h...  89.7 us
    unnamed x2, local copies, waits for them, and re-layouts  2.93 us

profile of v4, /device:TPU:0, one launch (start us, length us, event | category | flops | bytes accessed | tf_op | source)
XLA Modules:
  0.0 93.2 jit_solution(8560694380596263278)
XLA Ops:
  0.7 1.3 %copy.18.slot_images = s32[3,2]{1,0:T(4,128)} copy(s32[3,2]{0,1:T(2,128)} %param.19) | data formatting | bytes 48 | tf_op args[2]
  2.0 89.7 %shard_map.163 = bf16[1,196,384]{2,1,0:T(8,128)(2,1)} custom-call(s32[16]{0:T(128)} %image_slot.1, s32[3,2]{1,0:T(4,128)} %copy.18.slot_images, s32[1]{0:T(128)S(6)} %copy.20.slot_count, bf16[1,196,384]{2,1,0:T(8,128)(2,1)} %features.1, f32[1,768]{1,0:T(1,128)} %g_self.1, f32[1,768]{1,0:T(1,128)} %g_query.1, f32[1,768]{1,0:T(1,128)} %g_memory.1, ...), custom_call_target="tpu_custom_call" | custom-call | tf_op jit(solution)/shard_map/pallas_call | solution.py:598
  91.6 1.6 %copy.21 = bf16[1,196,384]{2,1,0:T(8,128)(2,1)} copy(bf16[1,196,384]{2,1,0:T(8,128)(2,1)} %shard_map.163) | data formatting | bytes 301056

commit v5 on v4

--- a/solution.py
+++ b/solution.py
@@ -40,7 +40,7 @@
     rows = q_ref.shape[0]
     low = lax.broadcasted_iota(jnp.int32, (rows, PAIR), 1) < HEAD_DIM
     for pair in range(width // PAIR):
-        if pair * PAIR == width // 2:
+        if comm is not None and pair * PAIR == width // 2:
             comm()
         q = q_ref[:, pair * PAIR : (pair + 1) * PAIR]
         k = k_ref[:, k_at + pair * PAIR : k_at + (pair + 1) * PAIR]
@@ -211,15 +211,9 @@
     feature_across = feature_out(own, x, 0, 1, 0)
     near_zero = [feature_out(block, 2, 1, 0, 1) for block in (own, passed)]
     near_one = [feature_out(block, 3, 1, 0, 2) for block in (passed, own)]
-    far_zero = [feature_out(block, WINDOW, 2, 0, 3) for block in (own, passed)]
+    far_zero = feature_out(own, WINDOW, 2, 0, 3)
     onto_next = feature_out(win.at[WINDOW, s], 2, -1, 0, 4)
-
-    def zero_start(at):
-        far_zero[at].start()
-
-        @pl.when(jnp.logical_not(even))
-        def _():
-            near_zero[at].start()
+    far_across = feature_out(win.at[WINDOW, s], WINDOW, 0, 1, 5)
 
     def relay(place, block=None):
         target = win.at[place, s]
@@ -234,7 +228,11 @@
 
     @pl.when(x == 0)
     def _():
-        zero_start(0)
+        far_zero.start()
+
+        @pl.when(jnp.logical_not(even))
+        def _():
+            near_zero[0].start()
 
     @pl.when(x == 1)
     def _():
@@ -288,34 +286,45 @@
         relay(place).start()
 
     group = kinds // 2
-    early = 3 * group
+    early = 5 * group
     pieces(0, group)
     arrived(1 - x)
 
     @pl.when(x == 0)
     def _():
         near_one[0].start()
+        arrived(WINDOW)
+
+        @pl.when(even)
+        def _():
+            onto_next.start()
+
+        far_across.start()
 
     @pl.when(x == 1)
     def _():
-        zero_start(1)
-
-    arrived(WINDOW)
-
-    @pl.when(even)
-    def _():
-        onto_next.start()
+        near_zero[1].start()
+
+    @pl.when(at_home)
+    def _():
+        weights_out[1].start()
 
     pieces(group, 2 * group)
     arrived(3)
+
+    @pl.when(x == 1)
+    def _():
+        arrived(WINDOW)
+
+    pieces(2 * group, 4 * group)
     arrived(2)
 
     @pl.when(at_home)
     def _():
-        for copy in weights_out[1:]:
+        for copy in weights_out[2:]:
             copy.start()
 
-    pieces(2 * group, early)
+    pieces(4 * group, early)
     own_win.wait()
     for place in range(REACH):
         block = win.at[place, 1 - s]
@@ -347,7 +356,7 @@
     def tokens_of(place):
         return jnp.concatenate([win[place, 0], win[place, 1]], axis=-1).astype(jnp.float32)
 
-    stops = 6 * slots
+    stops = 5 * slots
     each = max((total_pieces * 26 // 32 - early) // stops, 0)
     fronted = early + each * stops
 
@@ -355,7 +364,7 @@
         told = [0]
 
         def comm():
-            base = early + (6 * slot + told[0]) * each
+            base = early + (5 * slot + told[0]) * each
             told[0] += 1
             for at in range(each):
                 piece(base + at)
@@ -378,7 +387,7 @@
         queries[...] = matmul(query_in, m_query[...]).astype(jnp.bfloat16)
         kv[...] = matmul(memory_in, m_memory[...]).astype(jnp.bfloat16)
         comm()
-        attend(queries, kv, kv, 0, width, mixed, width, comm)
+        attend(queries, kv, kv, 0, width, mixed, width, None)
         first_wait(slot, 4)
         result = second[slot, 0:rows, :] + matmul(mixed[...], m_cross_out[...])
         second[slot, 0:rows, :] = result
@@ -530,14 +539,19 @@
         at = slice(comp * pix, (comp + 1) * pix)
         out[0, :, at] = (final[:, at] / conf).astype(jnp.bfloat16)
 
-    for copy in (feature_across, near_one[0], far_zero[0]):
+    for copy in (feature_across, near_one[0]):
         copy.wait_send()
 
-    @pl.when(even)
-    def _():
-        onto_next.wait_send()
-
-    @pl.when(jnp.logical_not(even))
+    @pl.when(x == 0)
+    def _():
+        far_zero.wait_send()
+        far_across.wait_send()
+
+        @pl.when(even)
+        def _():
+            onto_next.wait_send()
+
+    @pl.when(jnp.logical_or(x == 1, jnp.logical_not(even)))
     def _():
         near_zero[0].wait_send()
 
@@ -625,7 +639,7 @@
             pltpu.VMEM((4, rows, half), bf16),
             pltpu.VMEM((4, rows, half), bf16),
             pltpu.VMEM((rows, half), f32),
-            dma, dma((5,)), dma((REACH,)), dma((REACH,)), dma((REACH,)),
+            dma, dma((6,)), dma((REACH,)), dma((REACH,)), dma((REACH,)),
             dma((2,)), dma((2,)), dma((5,)), dma((5,)), dma((7,)), dma((7,)),
             dma((kinds,)), dma((chips, kinds)), dma((chips, kinds)), dma((chips, kinds)),
             dma((chips, kinds)), dma((slots,)), dma((slots,)), dma((4,)), dma((4,)),

time: 93.4 us -> 90.4 us (0.968)
  Pallas kernels: 89.7 us -> 86.6 us
    pallas_call x1, Pallas kernels: 89.7 us -> 86.6 us  [on_device(): pl.pallas_call(decoder_kernel, out_shape=jax.ShapeDtypeStruct((1, rows, h...]
where the time goes in v5:
time: 90.4 us; the launch traced here: 90.2 us
  Pallas kernels  86.6 us (96%)
  local copies, waits for them, and re-layouts  2.93 us (3%)
    pallas_call x1, Pallas kernels, on_device(): pl.pallas_call(decoder_kernel, out_shape=jax.ShapeDtypeStruct((1, rows, h...  86.6 us
    unnamed x2, local copies, waits for them, and re-layouts  2.93 us

profile of v5, /device:TPU:0, one launch (start us, length us, event | category | flops | bytes accessed | tf_op | source)
XLA Modules:
  0.0 90.2 jit_solution(7877360708804426187)
XLA Ops:
  0.7 1.3 %copy.18.slot_images = s32[3,2]{1,0:T(4,128)} copy(s32[3,2]{0,1:T(2,128)} %param.19) | data formatting | bytes 48 | tf_op args[2]
  2.0 86.6 %shard_map.163 = bf16[1,196,384]{2,1,0:T(8,128)(2,1)} custom-call(s32[16]{0:T(128)} %image_slot.1, s32[3,2]{1,0:T(4,128)} %copy.18.slot_images, s32[1]{0:T(128)S(6)} %copy.20.slot_count, bf16[1,196,384]{2,1,0:T(8,128)(2,1)} %features.1, f32[1,768]{1,0:T(1,128)} %g_self.1, f32[1,768]{1,0:T(1,128)} %g_query.1, f32[1,768]{1,0:T(1,128)} %g_memory.1, ...), custom_call_target="tpu_custom_call" | custom-call | tf_op jit(solution)/shard_map/pallas_call | solution.py:612
  88.6 1.6 %copy.21 = bf16[1,196,384]{2,1,0:T(8,128)(2,1)} copy(bf16[1,196,384]{2,1,0:T(8,128)(2,1)} %shard_map.163) | data formatting | bytes 301056

commit v6 on v5

--- a/solution.py
+++ b/solution.py
@@ -85,11 +85,10 @@
     width = m_qkv.shape[0]
     slots = second.shape[0]
     tall = second.shape[1]
-    per = chips // BLOCKS
-    shard = ring_w.shape[2]
-    split = 2 if shard % 32 == 0 else 1
+    shard = w_fc1.shape[1]
+    rank = ring_w.shape[2]
+    split = shard // rank
     kinds = 2 * split
-    rank = shard // split
     total_pieces = kinds * chips
 
     sibling = (here, 1 - s)
@@ -122,14 +121,8 @@
     gain_refs = (g_self, g_query, g_memory, g_mlp, g_head)
     fcs = (w_fc1, w_fc2)
 
-    def slot_at(step, ring):
-        return 2 * step + ring
-
     def ring_view(step, kind, ring):
-        place = ring_w.at[lax.rem(kind, 2), slot_at(step, ring)]
-        if split == 1:
-            return place
-        return place.at[pl.ds(pl.multiple_of(lax.div(kind, 2) * rank, rank), rank)]
+        return ring_w.at[lax.rem(kind, 2), 2 * (split * step + lax.div(kind, 2)) + ring]
 
     def own_fc(which, piece):
         if split == 1:
@@ -246,10 +239,17 @@
             copy.start()
         weights_out[0].start()
 
+    swapped = len(fc_out) // 2
+
     @pl.when(jnp.logical_not(at_home))
     def _():
-        for copy in fc_out:
+        for copy in fc_out[:swapped]:
             copy.start()
+
+        @pl.when(x == 1)
+        def _():
+            for copy in fc_out[swapped:]:
+                copy.start()
 
     def piece(number):
         turn = lax.div(number, kinds // 2)
@@ -300,6 +300,11 @@
             onto_next.start()
 
         far_across.start()
+
+        @pl.when(jnp.logical_not(at_home))
+        def _():
+            for copy in fc_out[swapped:]:
+                copy.start()
 
     @pl.when(x == 1)
     def _():
@@ -399,20 +404,21 @@
     hidden[...] = jnp.zeros_like(hidden)
     lax.fori_loop(0, slots, front, 0)
 
-    def relayed(first, steps):
+    def relayed(first, count):
         def body(at, carry):
-            step, kind = first + lax.div(at, kinds), lax.rem(at, kinds)
+            turn, which = first + lax.div(at, 2), lax.rem(at, 2)
+            step, kind = lax.div(turn, split), 2 * lax.rem(turn, split) + which
             view = ring_view(step, kind, 1 - s)
             pltpu.make_async_copy(view, view, x_recv.at[step, kind]).wait()
             return carry
 
-        lax.fori_loop(0, steps * kinds, body, 0)
-
-    def expand(first, steps, slot):
-        count = 2 * steps
-        if shard % 16 == 0:
+        lax.fori_loop(0, 2 * count, body, 0)
+
+    def expand(first, turns, slot):
+        count = 2 * turns
+        if rank % 16 == 0:
             groups = [
-                [ring_w[f, pl.ds(2 * first, count)].reshape(count * shard, width) for f in range(2)]
+                [ring_w[f, pl.ds(2 * first, count)].reshape(count * rank, width) for f in range(2)]
             ]
         else:
             groups = [[ring_w[f, 2 * first + at] for f in range(2)] for at in range(count)]
@@ -423,6 +429,8 @@
             total = total + matmul(act, fc2)
         second[slot] = total
 
+    turns = split * chips
+    span = turns // BLOCKS
     whole = total_pieces - group
     left = whole - fronted
     places = (BLOCKS - 1) * slots
@@ -433,19 +441,19 @@
 
         @pl.when(slot == 0)
         def _():
-            relayed(block * per, per)
-
-        expand(block * per, per, slot)
+            relayed(block * span, span)
+
+        expand(block * span, span, slot)
         pieces(
             fronted + jnp.minimum(turn * rate, left), fronted + jnp.minimum((turn + 1) * rate, left)
         )
         return carry
 
     lax.fori_loop(0, places, expand_early, 0)
-    relayed((BLOCKS - 1) * per, per - 1)
+    relayed((BLOCKS - 1) * span, span - 1)
 
     def expand_late(slot, carry):
-        expand((BLOCKS - 1) * per, per - 1, slot)
+        expand((BLOCKS - 1) * span, span - 1, slot)
         pieces(
             whole + lax.div(slot * group, slots), whole + lax.div((slot + 1) * group, slots)
         )
@@ -454,7 +462,7 @@
     lax.fori_loop(0, slots, expand_late, 0)
     weight_wait(5)
     weight_wait(6)
-    relayed(chips - 1, 1)
+    relayed(turns - 1, 1)
     pix = half // 4
 
     def terms(slot, which, target):
@@ -471,7 +479,7 @@
         )
 
     def expand_last(slot, carry):
-        expand(chips - 1, 1, slot)
+        expand(turns - 1, 1, slot)
         hidden[slot] = layer_norm(second[slot], gains[4]).astype(jnp.bfloat16)
         terms(slot, 1 - s, term_away)
         away(slot).start()
@@ -492,52 +500,66 @@
         for slot in range(slots):
             sources.append((place_of(slot, x, core), slot < live, ref, slot))
 
-    def sums_of(place):
-        sums = jnp.zeros((rows, half), jnp.float32)
+    quarter = half // 2
+
+    def sums_of(place, part):
+        sums = jnp.zeros((rows, quarter), jnp.float32)
         for to, live, ref, slot in sources:
             chosen = jnp.logical_and(to == place, live)
-            sums = sums + jnp.where(chosen, ref[slot].astype(jnp.float32), 0.0)
+            value = ref[slot, :, part * quarter : (part + 1) * quarter].astype(jnp.float32)
+            sums = sums + jnp.where(chosen, value, 0.0)
         return sums
 
-    def far_copy(at, step, flip):
+    def far_copy(at, part, step, flip):
         return remote(
-            far_out.at[at], far_in.at[at], b_send.at[at], b_recv.at[at], (pair_of(step, flip), s)
+            far_out.at[at, part], far_in.at[at, part], b_send.at[at, part], b_recv.at[at, part],
+            (pair_of(step, flip), s),
         )
 
-    def far_send(at, step, flip, sums):
-        far_out[at] = sums.astype(jnp.bfloat16)
-        far_copy(at, step, flip).start()
-
-    def far_wait(at):
-        block = far_in.at[at]
-        pltpu.make_async_copy(block, block, b_recv.at[at]).wait()
+    def far_send(at, part, step, flip, sums):
+        far_out[at, part] = sums.astype(jnp.bfloat16)
+        far_copy(at, part, step, flip).start()
+
+    def far_wait(at, part):
+        block = far_in.at[at, part]
+        pltpu.make_async_copy(block, block, b_recv.at[at, part]).wait()
         return block[...].astype(jnp.float32)
 
-    far_send(0, 2, 0, sums_of(WINDOW))
-    far_send(1, 0, 1, sums_of(3 - x))
+    for part in range(2):
+        far_send(1, part, 0, 1, sums_of(3 - x, part))
+    for part in range(2):
+        far_send(0, part, 2, 0, sums_of(WINDOW, part))
 
     @pl.when(x == 0)
     def _():
-        far_send(3, 0, 1, sums_of(1))
-
-    final[...] = sums_of(2 + x)
-    far_send(2, 1, 0, final[...] + far_wait(1))
-    final[...] = sums_of(x)
+        for part in range(2):
+            far_send(3, part, 0, 1, sums_of(1, part))
+
+    for part in range(2):
+        final[part] = sums_of(2 + x, part)
+    for part in range(2):
+        far_send(2, part, 1, 0, final[part] + far_wait(1, part))
+    for part in range(2):
+        final[part] = sums_of(x, part)
 
     @pl.when(x == 1)
     def _():
-        far_send(3, 0, 1, sums_of(0) + far_wait(0))
+        for part in range(2):
+            far_send(3, part, 0, 1, sums_of(0, part) + far_wait(0, part))
 
     @pl.when(x == 0)
     def _():
-        final[...] = final[...] + far_wait(0)
-
-    final[...] = final[...] + far_wait(2)
-    final[...] = final[...] + far_wait(3)
-    conf = jnp.maximum(final[:, 3 * pix :], 1.0)
+        for part in range(2):
+            final[part] = final[part] + far_wait(0, part)
+
+    for part in range(2):
+        final[part] = final[part] + far_wait(2, part)
+    for part in range(2):
+        final[part] = final[part] + far_wait(3, part)
+    conf = jnp.maximum(final[1, :, pix:], 1.0)
     for comp in range(3):
-        at = slice(comp * pix, (comp + 1) * pix)
-        out[0, :, at] = (final[:, at] / conf).astype(jnp.bfloat16)
+        value = final[comp // 2, :, comp % 2 * pix : (comp % 2 + 1) * pix]
+        out[0, :, comp * pix : (comp + 1) * pix] = (value / conf).astype(jnp.bfloat16)
 
     for copy in (feature_across, near_one[0]):
         copy.wait_send()
@@ -588,7 +610,8 @@
     for slot in range(slots):
         away(slot).wait_send()
     for at, (step, flip) in enumerate(((2, 0), (0, 1), (1, 0), (0, 1))):
-        far_copy(at, step, flip).wait_send()
+        for part in range(2):
+            far_copy(at, part, step, flip).wait_send()
 
 
 def on_device(
@@ -604,7 +627,8 @@
     slots = slot_images.shape[0]
     tall = padded(rows)
     shard = w_fc1.shape[1]
-    kinds = 2 * (2 if shard % 32 == 0 else 1)
+    split = 2 if shard % 32 == 0 else 1
+    kinds = 2 * split
     half = w_head.shape[2] // 2
     bf16, f32 = jnp.bfloat16, jnp.float32
     dma = pltpu.SemaphoreType.DMA
@@ -625,7 +649,7 @@
             pltpu.VMEM(w_memory.shape[1:], bf16),
             pltpu.VMEM(w_cross_out.shape[1:], bf16),
             pltpu.VMEM((2, width, half), bf16),
-            pltpu.VMEM((2, devices, shard, width), bf16),
+            pltpu.VMEM((2, devices * split, shard // split, width), bf16),
             pltpu.VMEM((rows, 3 * width), bf16),
             pltpu.VMEM((rows, 2 * width), bf16),
             pltpu.VMEM((rows, width), bf16),
@@ -636,13 +660,13 @@
             pltpu.VMEM((slots, rows, half), f32),
             pltpu.VMEM((slots, rows, half), bf16),
             pltpu.VMEM((slots, rows, half), bf16),
-            pltpu.VMEM((4, rows, half), bf16),
-            pltpu.VMEM((4, rows, half), bf16),
-            pltpu.VMEM((rows, half), f32),
+            pltpu.VMEM((4, 2, rows, half // 2), bf16),
+            pltpu.VMEM((4, 2, rows, half // 2), bf16),
+            pltpu.VMEM((2, rows, half // 2), f32),
             dma, dma((6,)), dma((REACH,)), dma((REACH,)), dma((REACH,)),
             dma((2,)), dma((2,)), dma((5,)), dma((5,)), dma((7,)), dma((7,)),
             dma((kinds,)), dma((chips, kinds)), dma((chips, kinds)), dma((chips, kinds)),
-            dma((chips, kinds)), dma((slots,)), dma((slots,)), dma((4,)), dma((4,)),
+            dma((chips, kinds)), dma((slots,)), dma((slots,)), dma((4, 2)), dma((4, 2)),
         ],
         compiler_params=pltpu.CompilerParams(
             collective_id=0, has_side_effects=True, vmem_limit_bytes=VMEM_LIMIT

time: 90.4 us -> 90.4 us (level)
  no operation moved by 1% of the time
where the time goes in v6:
time: 90.4 us; the launch traced here: 90.2 us
  Pallas kernels  86.7 us (96%)
  local copies, waits for them, and re-layouts  2.93 us (3%)
    pallas_call x1, Pallas kernels, on_device(): pl.pallas_call(decoder_kernel, out_shape=jax.ShapeDtypeStruct((1, rows, h...  86.7 us
    unnamed x2, local copies, waits for them, and re-layouts  2.93 us

profile of v6, /device:TPU:0, one launch (start us, length us, event | category | flops | bytes accessed | tf_op | source)
XLA Modules:
  0.0 90.2 jit_solution(8370131538344746522)
XLA Ops:
  0.7 1.3 %copy.18.slot_images = s32[3,2]{1,0:T(4,128)} copy(s32[3,2]{0,1:T(2,128)} %param.19) | data formatting | bytes 48 | tf_op args[2]
  2.0 86.7 %shard_map.163 = bf16[1,196,384]{2,1,0:T(8,128)(2,1)} custom-call(s32[16]{0:T(128)} %image_slot.1, s32[3,2]{1,0:T(4,128)} %copy.18.slot_images, s32[1]{0:T(128)S(6)} %copy.20.slot_count, bf16[1,196,384]{2,1,0:T(8,128)(2,1)} %features.1, f32[1,768]{1,0:T(1,128)} %g_self.1, f32[1,768]{1,0:T(1,128)} %g_query.1, f32[1,768]{1,0:T(1,128)} %g_memory.1, ...), custom_call_target="tpu_custom_call" | custom-call | tf_op jit(solution)/shard_map/pallas_call | solution.py:636
  88.6 1.6 %copy.21 = bf16[1,196,384]{2,1,0:T(8,128)(2,1)} copy(bf16[1,196,384]{2,1,0:T(8,128)(2,1)} %shard_map.163) | data formatting | bytes 301056

commit v7 on v6

--- a/solution.py
+++ b/solution.py
@@ -349,8 +349,8 @@
             weight_wait(at)
 
     def entry(slot, column, core):
-        local = slot_images[slot, column]
-        return jnp.where(x == core, local, table[slot, column])
+        local = slot_images[column, slot]
+        return jnp.where(x == core, local, table[column, slot])
 
     def place_of(slot, column, core=None):
         core = s if core is None else core
@@ -635,12 +635,12 @@
     anywhere = pl.BlockSpec(memory_space=pl.ANY)
     return pl.pallas_call(
         decoder_kernel,
-        out_shape=jax.ShapeDtypeStruct((1, rows, half * 3 // 4), bf16),
+        out_shape=pltpu.VMEM((1, rows, half * 3 // 4), bf16),
         in_specs=[pl.BlockSpec(memory_space=pltpu.SMEM)] * 3 + [anywhere] * 14,
         out_specs=pl.BlockSpec(memory_space=pltpu.VMEM),
         scratch_shapes=[
             pltpu.VMEM((REACH, 2, rows, part), bf16),
-            pltpu.SMEM(slot_images.shape, jnp.int32),
+            pltpu.SMEM(slot_images.shape[::-1], jnp.int32),
             pltpu.SMEM(slot_count.shape, jnp.int32),
             pltpu.VMEM((5, 1, width), f32),
             pltpu.VMEM(w_qkv.shape[1:], bf16),
@@ -672,7 +672,7 @@
             collective_id=0, has_side_effects=True, vmem_limit_bytes=VMEM_LIMIT
         ),
     )(
-        image_slot, slot_images, slot_count, features, gain_self, gain_query, gain_memory,
+        image_slot, slot_images.T, slot_count, features, gain_self, gain_query, gain_memory,
         gain_mlp, gain_head, w_qkv, w_self_out, w_query, w_memory, w_cross_out, w_fc1, w_fc2,
         w_head,
     )

time: 90.4 us -> 87.5 us (0.968)
  local copies, waits for them, and re-layouts: 2.93 us -> 0.67 us
    unnamed x2 -> x1, local copies, waits for them, and re-layouts: 2.93 us -> 0.67 us
where the time goes in v7:
time: 87.5 us; the launch traced here: 87.3 us
  Pallas kernels  86 us (98%)
    pallas_call x1, Pallas kernels, on_device(): pl.pallas_call(decoder_kernel, out_shape=pltpu.VMEM((1, rows, half * 3 //...  86 us

profile of v7, /device:TPU:0, one launch (start us, length us, event | category | flops | bytes accessed | tf_op | source)
XLA Modules:
  0.0 87.3 jit_solution(664161571730957733)
XLA Ops:
  0.7 86.0 %shard_map.163 = bf16[1,196,384]{2,1,0:T(8,128)(2,1)S(1)} custom-call(s32[16]{0:T(128)} %image_slot.1, s32[2,3]{1,0:T(2,128)} %bitcast.1, s32[1]{0:T(128)S(6)} %copy.20.slot_count, bf16[1,196,384]{2,1,0:T(8,128)(2,1)} %features.1, f32[1,768]{1,0:T(1,128)} %g_self.1, f32[1,768]{1,0:T(1,128)} %g_query.1, f32[1,768]{1,0:T(1,128)} %g_memory.1, f32[1,768]{1,0:T(1,128)} %g_mlp.1, ...), custom_call_target="tpu_custom_call" | custom-call | tf_op jit(solution)/shard_map/pallas_call | solution.py:636
  86.7 0.7 copy.19

commit v8 on v7

--- a/solution.py
+++ b/solution.py
@@ -361,7 +361,7 @@
     def tokens_of(place):
         return jnp.concatenate([win[place, 0], win[place, 1]], axis=-1).astype(jnp.float32)
 
-    stops = 5 * slots
+    stops = 4 * slots
     each = max((total_pieces * 26 // 32 - early) // stops, 0)
     fronted = early + each * stops
 
@@ -369,7 +369,7 @@
         told = [0]
 
         def comm():
-            base = early + (5 * slot + told[0]) * each
+            base = early + (4 * slot + told[0]) * each
             told[0] += 1
             for at in range(each):
                 piece(base + at)
@@ -379,7 +379,7 @@
         state = layer_norm(tokens, gains[0]).astype(jnp.bfloat16)
         triple[...] = matmul(state, m_qkv[...]).astype(jnp.bfloat16)
         comm()
-        attend(triple, triple, triple, width, 2 * width, mixed, width, comm)
+        attend(triple, triple, triple, width, 2 * width, mixed, width, None)
         first_wait(slot, 1)
         first = tokens + matmul(mixed[...], m_self_out[...])
         second[slot, 0:rows, :] = first
@@ -391,8 +391,7 @@
         memory_in = layer_norm(memory, gains[2]).astype(jnp.bfloat16)
         queries[...] = matmul(query_in, m_query[...]).astype(jnp.bfloat16)
         kv[...] = matmul(memory_in, m_memory[...]).astype(jnp.bfloat16)
-        comm()
-        attend(queries, kv, kv, 0, width, mixed, width, None)
+        attend(queries, kv, kv, 0, width, mixed, width, comm)
         first_wait(slot, 4)
         result = second[slot, 0:rows, :] + matmul(mixed[...], m_cross_out[...])
         second[slot, 0:rows, :] = result
@@ -434,7 +433,7 @@
     whole = total_pieces - group
     left = whole - fronted
     places = (BLOCKS - 1) * slots
-    rate = -(-left // (2 * slots))
+    pace = BLOCKS * slots
 
     def expand_early(turn, carry):
         block, slot = lax.div(turn, slots), lax.rem(turn, slots)
@@ -445,11 +444,12 @@
 
         expand(block * span, span, slot)
         pieces(
-            fronted + jnp.minimum(turn * rate, left), fronted + jnp.minimum((turn + 1) * rate, left)
+            fronted + lax.div(turn * left, pace), fronted + lax.div((turn + 1) * left, pace)
         )
         return carry
 
     lax.fori_loop(0, places, expand_early, 0)
+    pieces(fronted + places * left // pace, whole)
     relayed((BLOCKS - 1) * span, span - 1)
 
     def expand_late(slot, carry):

time: 87.5 us -> 84.7 us (0.968)
  Pallas kernels: 86 us -> 83.2 us
    pallas_call x1, Pallas kernels: 86 us -> 83.2 us  [on_device(): pl.pallas_call(decoder_kernel, out_shape=pltpu.VMEM((1, rows, half * 3 //...]
where the time goes in v8:
time: 84.7 us; the launch traced here: 84.5 us
  Pallas kernels  83.2 us (98%)
    pallas_call x1, Pallas kernels, on_device(): pl.pallas_call(decoder_kernel, out_shape=pltpu.VMEM((1, rows, half * 3 //...  83.2 us

profile of v8, /device:TPU:0, one launch (start us, length us, event | category | flops | bytes accessed | tf_op | source)
XLA Modules:
  0.0 84.5 jit_solution(16829984554375962486)
XLA Ops:
  0.7 83.2 %shard_map.163 = bf16[1,196,384]{2,1,0:T(8,128)(2,1)S(1)} custom-call(s32[16]{0:T(128)} %image_slot.1, s32[2,3]{1,0:T(2,128)} %bitcast.1, s32[1]{0:T(128)S(6)} %copy.20.slot_count, bf16[1,196,384]{2,1,0:T(8,128)(2,1)} %features.1, f32[1,768]{1,0:T(1,128)} %g_self.1, f32[1,768]{1,0:T(1,128)} %g_query.1, f32[1,768]{1,0:T(1,128)} %g_memory.1, f32[1,768]{1,0:T(1,128)} %g_mlp.1, ...), custom_call_target="tpu_custom_call" | custom-call | tf_op jit(solution)/shard_map/pallas_call | solution.py:636
  83.8 0.7 copy.19

commit v9 on v8

--- a/solution.py
+++ b/solution.py
@@ -215,6 +215,11 @@
             sibling,
         )
 
+    @pl.when(at_home)
+    def _():
+        for copy in fc_home:
+            copy.start()
+
     for copy in table_out:
         copy.start()
     feature_across.start()
@@ -235,7 +240,7 @@
 
     @pl.when(at_home)
     def _():
-        for copy in fc_home + gains_out:
+        for copy in gains_out:
             copy.start()
         weights_out[0].start()
 
@@ -452,10 +457,13 @@
     pieces(fronted + places * left // pace, whole)
     relayed((BLOCKS - 1) * span, span - 1)
 
+    early_rate = -(-group // (slots - 1))
+
     def expand_late(slot, carry):
         expand((BLOCKS - 1) * span, span - 1, slot)
         pieces(
-            whole + lax.div(slot * group, slots), whole + lax.div((slot + 1) * group, slots)
+            whole + jnp.minimum(slot * early_rate, group),
+            whole + jnp.minimum((slot + 1) * early_rate, group),
         )
         return carry
 
@@ -489,8 +497,10 @@
         terms(slot, s, term)
         return carry
 
-    lax.fori_loop(0, slots, expand_last, 0)
-    lax.fori_loop(0, slots, own_terms, 0)
+    for slot in range(slots):
+        expand_last(slot, 0)
+    for slot in range(slots):
+        own_terms(slot, 0)
     for slot in range(slots):
         away(slot).wait_recv()
 
@@ -535,6 +545,52 @@
         for part in range(2):
             far_send(3, part, 0, 1, sums_of(1, part))
 
+    for copy in (feature_across, near_one[0]):
+        copy.wait_send()
+
+    @pl.when(x == 0)
+    def _():
+        far_zero.wait_send()
+        far_across.wait_send()
+
+        @pl.when(even)
+        def _():
+            onto_next.wait_send()
+
+    @pl.when(jnp.logical_or(x == 1, jnp.logical_not(even)))
+    def _():
+        near_zero[0].wait_send()
+
+    for place in range(REACH):
+        relay(place).wait_send()
+
+    @pl.when(at_home)
+    def _():
+        for copy in fc_home + gains_out + weights_out:
+            copy.wait_send()
+
+    @pl.when(jnp.logical_not(at_home))
+    def _():
+        for copy in fc_out:
+            copy.wait_send()
+
+    for copy in table_out:
+        copy.wait_send()
+
+    def drain(number, carry):
+        step, kind = lax.div(number, kinds), lax.rem(number, kinds)
+        block = ring_view(step, kind, s)
+
+        @pl.when(step < chips - 1)
+        def _():
+            remote(
+                block, block, r_send.at[step, kind], r_recv.at[step, kind], onward
+            ).wait_send()
+
+        remote(block, block, x_send.at[step, kind], x_recv.at[step, kind], sibling).wait_send()
+        return carry
+
+    lax.fori_loop(0, total_pieces, drain, 0)
     for part in range(2):
         final[part] = sums_of(2 + x, part)
     for part in range(2):
@@ -561,52 +617,6 @@
         value = final[comp // 2, :, comp % 2 * pix : (comp % 2 + 1) * pix]
         out[0, :, comp * pix : (comp + 1) * pix] = (value / conf).astype(jnp.bfloat16)
 
-    for copy in (feature_across, near_one[0]):
-        copy.wait_send()
-
-    @pl.when(x == 0)
-    def _():
-        far_zero.wait_send()
-        far_across.wait_send()
-
-        @pl.when(even)
-        def _():
-            onto_next.wait_send()
-
-    @pl.when(jnp.logical_or(x == 1, jnp.logical_not(even)))
-    def _():
-        near_zero[0].wait_send()
-
-    for place in range(REACH):
-        relay(place).wait_send()
-
-    @pl.when(at_home)
-    def _():
-        for copy in fc_home + gains_out + weights_out:
-            copy.wait_send()
-
-    @pl.when(jnp.logical_not(at_home))
-    def _():
-        for copy in fc_out:
-            copy.wait_send()
-
-    for copy in table_out:
-        copy.wait_send()
-
-    def drain(number, carry):
-        step, kind = lax.div(number, kinds), lax.rem(number, kinds)
-        block = ring_view(step, kind, s)
-
-        @pl.when(step < chips - 1)
-        def _():
-            remote(
-                block, block, r_send.at[step, kind], r_recv.at[step, kind], onward
-            ).wait_send()
-
-        remote(block, block, x_send.at[step, kind], x_recv.at[step, kind], sibling).wait_send()
-        return carry
-
-    lax.fori_loop(0, total_pieces, drain, 0)
     for slot in range(slots):
         away(slot).wait_send()
     for at, (step, flip) in enumerate(((2, 0), (0, 1), (1, 0), (0, 1))):

time: 84.7 us -> 83.5 us (0.986)
  Pallas kernels: 83.2 us -> 82 us
    pallas_call x1, Pallas kernels: 83.2 us -> 82 us  [on_device(): pl.pallas_call(decoder_kernel, out_shape=pltpu.VMEM((1, rows, half * 3 //...]
where the time goes in v9:
time: 83.5 us; the launch traced here: 83.3 us
  Pallas kernels  82 us (98%)
    pallas_call x1, Pallas kernels, on_device(): pl.pallas_call(decoder_kernel, out_shape=pltpu.VMEM((1, rows, half * 3 //...  82 us

profile of v9, /device:TPU:0, one launch (start us, length us, event | category | flops | bytes accessed | tf_op | source)
XLA Modules:
  0.0 83.3 jit_solution(14791508382982572137)
XLA Ops:
  0.7 82.0 %shard_map.163 = bf16[1,196,384]{2,1,0:T(8,128)(2,1)S(1)} custom-call(s32[16]{0:T(128)} %image_slot.1, s32[2,3]{1,0:T(2,128)} %bitcast.1, s32[1]{0:T(128)S(6)} %copy.20.slot_count, bf16[1,196,384]{2,1,0:T(8,128)(2,1)} %features.1, f32[1,768]{1,0:T(1,128)} %g_self.1, f32[1,768]{1,0:T(1,128)} %g_query.1, f32[1,768]{1,0:T(1,128)} %g_memory.1, f32[1,768]{1,0:T(1,128)} %g_mlp.1, ...), custom_call_target="tpu_custom_call" | custom-call | tf_op jit(solution)/shard_map/pallas_call | solution.py:646
  82.6 0.7 copy.19

commit v10 on v9

--- a/solution.py
+++ b/solution.py
@@ -487,7 +487,6 @@
         )
 
     def expand_last(slot, carry):
-        expand(turns - 1, 1, slot)
         hidden[slot] = layer_norm(second[slot], gains[4]).astype(jnp.bfloat16)
         terms(slot, 1 - s, term_away)
         away(slot).start()
@@ -497,6 +496,13 @@
         terms(slot, s, term)
         return carry
 
+    joined = hidden[...].reshape(slots * tall, width)
+    for unit in range(2 * (turns - 1), 2 * turns) if rank % 16 else (None,):
+        units = pl.ds(2 * (turns - 1), 2) if unit is None else pl.ds(unit, 1)
+        fc1, fc2 = [ring_w[f, units].reshape(-1, width) for f in range(2)]
+        pre = matmul_t(joined, fc1)
+        act = (pre * (1.0 + lax.erf(pre * 0.5**0.5)) * 0.5).astype(jnp.bfloat16)
+        second[...] = second[...] + matmul(act, fc2).reshape(slots, tall, width)
     for slot in range(slots):
         expand_last(slot, 0)
     for slot in range(slots):

time: 83.5 us -> 82.9 us (level)
  no operation moved by 1% of the time
where the time goes in v10:
time: 82.9 us; the launch traced here: 82.7 us
  Pallas kernels  81.4 us (98%)
    pallas_call x1, Pallas kernels, on_device(): pl.pallas_call(decoder_kernel, out_shape=pltpu.VMEM((1, rows, half * 3 //...  81.4 us

profile of v10, /device:TPU:0, one launch (start us, length us, event | category | flops | bytes accessed | tf_op | source)
XLA Modules:
  0.0 82.7 jit_solution(953987387741008059)
XLA Ops:
  0.7 81.4 %shard_map.163 = bf16[1,196,384]{2,1,0:T(8,128)(2,1)S(1)} custom-call(s32[16]{0:T(128)} %image_slot.1, s32[2,3]{1,0:T(2,128)} %bitcast.1, s32[1]{0:T(128)S(6)} %copy.20.slot_count, bf16[1,196,384]{2,1,0:T(8,128)(2,1)} %features.1, f32[1,768]{1,0:T(1,128)} %g_self.1, f32[1,768]{1,0:T(1,128)} %g_query.1, f32[1,768]{1,0:T(1,128)} %g_memory.1, f32[1,768]{1,0:T(1,128)} %g_mlp.1, ...), custom_call_target="tpu_custom_call" | custom-call | tf_op jit(solution)/shard_map/pallas_call | solution.py:652
  82.1 0.7 copy.19

commit v11 on v10

--- a/solution.py
+++ b/solution.py
@@ -146,7 +146,7 @@
     barrier = pltpu.get_barrier_semaphore()
     for step in range(-2, 3):
         for flip in range(2):
-            if step or flip:
+            if (step == 0) == (flip == 1):
                 pl.semaphore_signal(
                     barrier, inc=1, device_id=(pair_of(step, flip), s), device_id_type=MESH
                 )
@@ -156,7 +156,7 @@
     def _():
         pl.semaphore_signal(barrier, inc=1, device_id=partner, device_id_type=MESH)
 
-    pl.semaphore_wait(barrier, 10 + (1 - at_home.astype(jnp.int32)))
+    pl.semaphore_wait(barrier, 6 + (1 - at_home.astype(jnp.int32)))
 
     table_out = [
         remote(slot_images, table, t_send.at[0], t_recv.at[0], (pair_of(0, 1), s)),
@@ -236,7 +236,12 @@
     def _():
         near_one[1].start()
 
-    relay(x, own).start()
+    def wanted(place):
+        return jnp.logical_and(place >= 1 - s, place <= WINDOW - s)
+
+    @pl.when(wanted(x))
+    def _():
+        relay(x, own).start()
 
     @pl.when(at_home)
     def _():
@@ -288,7 +293,10 @@
     def arrived(place):
         block = win.at[place, s]
         pltpu.make_async_copy(block, block, f_recv.at[place]).wait()
-        relay(place).start()
+
+        @pl.when(wanted(place))
+        def _():
+            relay(place).start()
 
     group = kinds // 2
     early = 5 * group
@@ -336,7 +344,7 @@
 
     pieces(4 * group, early)
     own_win.wait()
-    for place in range(REACH):
+    for place in [s + ahead for ahead in range(WINDOW)]:
         block = win.at[place, 1 - s]
         pltpu.make_async_copy(block, block, fr_recv.at[place]).wait()
     for copy in table_out:
@@ -567,7 +575,7 @@
     def _():
         near_zero[0].wait_send()
 
-    for place in range(REACH):
+    for place in [1 - s + ahead for ahead in range(WINDOW)]:
         relay(place).wait_send()
 
     @pl.when(at_home)

time: 82.9 us -> 82 us (0.989)
  Pallas kernels: 81.4 us -> 80.5 us
    pallas_call x1, Pallas kernels: 81.4 us -> 80.5 us  [on_device(): pl.pallas_call(decoder_kernel, out_shape=pltpu.VMEM((1, rows, half * 3 //...]
where the time goes in v11:
time: 82 us; the launch traced here: 81.8 us
  Pallas kernels  80.5 us (98%)
    pallas_call x1, Pallas kernels, on_device(): pl.pallas_call(decoder_kernel, out_shape=pltpu.VMEM((1, rows, half * 3 //...  80.5 us

profile of v11, /device:TPU:0, one launch (start us, length us, event | category | flops | bytes accessed | tf_op | source)
XLA Modules:
  0.0 81.8 jit_solution(5995668074665493748)
XLA Ops:
  0.7 80.5 %shard_map.163 = bf16[1,196,384]{2,1,0:T(8,128)(2,1)S(1)} custom-call(s32[16]{0:T(128)} %image_slot.1, s32[2,3]{1,0:T(2,128)} %bitcast.1, s32[1]{0:T(128)S(6)} %copy.20.slot_count, bf16[1,196,384]{2,1,0:T(8,128)(2,1)} %features.1, f32[1,768]{1,0:T(1,128)} %g_self.1, f32[1,768]{1,0:T(1,128)} %g_query.1, f32[1,768]{1,0:T(1,128)} %g_memory.1, f32[1,768]{1,0:T(1,128)} %g_mlp.1, ...), custom_call_target="tpu_custom_call" | custom-call | tf_op jit(solution)/shard_map/pallas_call | solution.py:660
  81.1 0.7 copy.19
